TPU v7x, 32 devices: a whole 2x2x4 slice. The times are simulated.
32 devices in a mesh: ez: 4 (over z), ey: 2 (over y), ex: 4 (over x, core).
Axes of the slice: x: 2, y: 2, z: 4, core: 2. Of those that a mesh axis runs over, the one named last changes fastest.
Arguments:
- tokens_in: bfloat16 [2, 8192, 1536], P(None, ('ez', 'ey', 'ex'))
- expert_ids: int32 [2, 2, 8192, 6], P(None, None, ('ez', 'ey', 'ex'))
- gate_vals: float32 [2, 2, 8192, 6], P(None, None, ('ez', 'ey', 'ex'))
- w_up1: bfloat16 [2, 64, 1536, 512], P(None, ('ez', 'ey', 'ex'))
- w_up3: bfloat16 [2, 64, 1536, 512], P(None, ('ez', 'ey', 'ex'))
- w_down: bfloat16 [2, 64, 512, 1536], P(None, ('ez', 'ey', 'ex'))
Outputs:
- output: bfloat16 [2, 8192, 1536], P(None, ('ez', 'ey', 'ex'))
All inputs are finite; a program needn't handle non-finite values.
Results may differ from a plain program's by a relative error of at most 0.0115358.
Values are sent between devices in bfloat16 or wider.
A program may use at most 1 GiB of HBM per device.

v0:
```python
import jax
import jax.numpy as jnp
from jax import lax
from jax.sharding import PartitionSpec as P

ROUTE_SCALE = 2.5
MESH_AXES = ("ez", "ey", "ex")


def capacity_of(tok_mb, top_k, experts):
    return 2 * ((tok_mb * top_k + experts - 1) // experts)


def slot_layout(ids_blk, gates_blk, first_slot, num_slots, experts, capacity):
    chosen = (ids_blk[..., None] == jnp.arange(experts)).astype(jnp.int32)
    per_expert = jnp.sum(chosen, axis=-2)
    token_rank = jnp.cumsum(per_expert, axis=-2) - per_expert
    slot_pos = jnp.sum(chosen * token_rank[..., None, :], axis=-1)
    flat_slot = ids_blk * capacity + slot_pos - first_slot
    slot_match = flat_slot[..., None] == jnp.arange(num_slots)
    dispatch = jnp.any(slot_match, axis=-2).astype(jnp.bfloat16)
    combine = jnp.sum(jnp.where(slot_match, gates_blk[..., None], 0.0), axis=-2)
    return dispatch, combine


def expert_ffn(expert_rows, mat_up1, mat_up3, mat_down):
    gate_in = jnp.einsum("eldi,lig->eldg", expert_rows, mat_up1, preferred_element_type=jnp.float32)
    lin_in = jnp.einsum("eldi,lig->eldg", expert_rows, mat_up3, preferred_element_type=jnp.float32)
    hidden = (jax.nn.silu(gate_in) * lin_in).astype(jnp.bfloat16)
    return jnp.einsum("dkcf,kfh->dkch", hidden, mat_down, preferred_element_type=jnp.float32).astype(jnp.bfloat16)


def solution(mesh):
    n_dev = mesh.shape["ez"] * mesh.shape["ey"] * mesh.shape["ex"]
    tok_spec = P(None, MESH_AXES, None)
    route_spec = P(None, None, MESH_AXES, None)
    weight_spec = P(None, MESH_AXES, None, None)

    def device_body(tokens_in, expert_ids, gate_vals, w_up1, w_up3, w_down):
        n_layers, n_micro, tok_mb, top_k = expert_ids.shape
        exp_dev = w_up1.shape[1]
        hidden_size = tokens_in.shape[-1]
        experts = exp_dev * n_dev
        capacity = capacity_of(tok_mb, top_k, experts)
        batches = [tokens_in[mb_idx] for mb_idx in range(n_micro)]
        for layer_idx in range(n_layers):
            for mb_idx in range(n_micro):
                tokens = batches[mb_idx]
                dispatch, combine = slot_layout(expert_ids[layer_idx, mb_idx], gate_vals[layer_idx, mb_idx], 0, experts * capacity, experts, capacity)
                send_buf = jnp.einsum("tn,th->nh", dispatch, tokens, preferred_element_type=jnp.float32).astype(jnp.bfloat16)
                send_buf = send_buf.reshape(n_dev, exp_dev, capacity, hidden_size)
                recv_buf = lax.all_to_all(send_buf, MESH_AXES, 0, 0, tiled=True)
                expert_out = expert_ffn(recv_buf, w_up1[layer_idx], w_up3[layer_idx], w_down[layer_idx])
                returned = lax.all_to_all(expert_out, MESH_AXES, 0, 0, tiled=True)
                moe_sum = jnp.dot(combine, returned.reshape(experts * capacity, hidden_size), preferred_element_type=jnp.float32)
                batches[mb_idx] = (tokens.astype(jnp.float32) + ROUTE_SCALE * moe_sum).astype(jnp.bfloat16)
        return jnp.stack(batches)

    return jax.shard_map(device_body, mesh=mesh, in_specs=(tok_spec, route_spec, route_spec, weight_spec, weight_spec, weight_spec), out_specs=tok_spec, check_vma=False)
```

profile of v0, /device:TPU:0, one launch (start us, length us, event | category | flops | bytes accessed | tf_op | source)
XLA Modules:
  0.0 1702.1 jit_solution(17892277606890957118)
XLA Ops:
  12.4 7.6 all-to-all-start
  30.5 187.6 %all-to-all-done = bf16[32,2,48,1536]{3,2,1,0:T(8,128)(2,1)} async-done(((bf16[32,2,48,1536]{3,2,1,0:T(8,128)(2,1)}), bf16[32,2,48,1536]{3,2,1,0:T(8,128)(2,1)}, u32[]{:S(2)}, u32[]{:S(2)}) %all-to-all-start) | async-done | bytes 9437216 | tf_op jit(solution)/shard_map/all_to_all | solution.py:52
  218.1 12.8 all-to-all-start.4
  230.9 11.1 fusion.16
  242.1 18.1 %convert_bitcast_fusion.3 = bf16[32,2,48,1536]{3,2,0,1:T(8,128)(2,1)} fusion(f32[2,32,48,512]{3,2,1,0:T(8,128)} %fusion.16, bf16[2,2,512,1536]{3,2,1,0:T(8,128)(2,1)} %param.11, bf16[32,2,48,1536]{3,2,1,0:T(8,128)(2,1)} %all-to-all-done, bf16[2,2,1536,512]{3,2,1,0:T(8,128)(2,1)} %param.9), kind=kOutput, calls=%fused_computation.19 | convolution fusion | flops 9677832192 | bytes 31457280 | tf_op jit(solution)/shard_map/dkcf,kfh->dkch/dot_general | solution.py:30
  260.1 8.2 copy.116
  268.4 160.7 %all-to-all-done.4 = bf16[32,2,48,1536]{3,2,1,0:T(8,128)(2,1)} async-done(((bf16[32,2,48,1536]{3,2,1,0:T(8,128)(2,1)}), bf16[32,2,48,1536]{3,2,1,0:T(8,128)(2,1)}, u32[]{:S(2)}, u32[]{:S(2)}) %all-to-all-start.4) | async-done | bytes 9437216 | tf_op jit(solution)/shard_map/all_to_all | solution.py:52
  429.0 12.9 all-to-all-start.1
  441.9 11.1 fusion.8
  453.0 18.1 %convert_bitcast_fusion.1 = bf16[32,2,48,1536]{3,2,0,1:T(8,128)(2,1)} fusion(f32[2,32,48,512]{3,2,1,0:T(8,128)} %fusion.8, bf16[2,2,512,1536]{3,2,1,0:T(8,128)(2,1)} %param.11, bf16[32,2,48,1536]{3,2,1,0:T(8,128)(2,1)} %all-to-all-done.4, bf16[2,2,1536,512]{3,2,1,0:T(8,128)(2,1)} %param.9), kind=kOutput, calls=%fused_computation.17 | convolution fusion | flops 9677832192 | bytes 31457280 | tf_op jit(solution)/shard_map/dkcf,kfh->dkch/dot_general | solution.py:30
  471.1 8.2 copy.130
  479.3 160.7 %all-to-all-done.1 = bf16[32,2,48,1536]{3,2,1,0:T(8,128)(2,1)} async-done(((bf16[32,2,48,1536]{3,2,1,0:T(8,128)(2,1)}), bf16[32,2,48,1536]{3,2,1,0:T(8,128)(2,1)}, u32[]{:S(2)}, u32[]{:S(2)}) %all-to-all-start.1) | async-done | bytes 9437216 | tf_op jit(solution)/shard_map/all_to_all | solution.py:54
  640.0 13.1 all-to-all-start.5
  662.6 6.4 fusion.75
  674.3 176.9 %all-to-all-done.5 = bf16[32,2,48,1536]{3,2,1,0:T(8,128)(2,1)} async-done(((bf16[32,2,48,1536]{3,2,1,0:T(8,128)(2,1)}), bf16[32,2,48,1536]{3,2,1,0:T(8,128)(2,1)}, u32[]{:S(2)}, u32[]{:S(2)}) %all-to-all-start.5) | async-done | bytes 9437216 | tf_op jit(solution)/shard_map/all_to_all | solution.py:54
  851.2 12.6 all-to-all-start.2
  873.3 6.3 fusion.73
  885.2 176.8 %all-to-all-done.2 = bf16[32,2,48,1536]{3,2,1,0:T(8,128)(2,1)} async-done(((bf16[32,2,48,1536]{3,2,1,0:T(8,128)(2,1)}), bf16[32,2,48,1536]{3,2,1,0:T(8,128)(2,1)}, u32[]{:S(2)}, u32[]{:S(2)}) %all-to-all-start.2) | async-done | bytes 9437216 | tf_op jit(solution)/shard_map/all_to_all | solution.py:52
  1062.0 12.5 all-to-all-start.6
  1074.6 11.1 fusion.12
  1085.7 18.1 %convert_bitcast_fusion.2 = bf16[32,2,48,1536]{3,2,0,1:T(8,128)(2,1)} fusion(f32[2,32,48,512]{3,2,1,0:T(8,128)} %fusion.12, bf16[2,2,512,1536]{3,2,1,0:T(8,128)(2,1)} %param.11, bf16[32,2,48,1536]{3,2,1,0:T(8,128)(2,1)} %all-to-all-done.2, bf16[2,2,1536,512]{3,2,1,0:T(8,128)(2,1)} %param.9), kind=kOutput, calls=%fused_computation.18 | convolution fusion | flops 9677832192 | bytes 31457280 | tf_op jit(solution)/shard_map/dkcf,kfh->dkch/dot_general | solution.py:30
  1103.8 8.2 copy.123
  1112.0 160.8 %all-to-all-done.6 = bf16[32,2,48,1536]{3,2,1,0:T(8,128)(2,1)} async-done(((bf16[32,2,48,1536]{3,2,1,0:T(8,128)(2,1)}), bf16[32,2,48,1536]{3,2,1,0:T(8,128)(2,1)}, u32[]{:S(2)}, u32[]{:S(2)}) %all-to-all-start.6) | async-done | bytes 9437216 | tf_op jit(solution)/shard_map/all_to_all | solution.py:52
  1272.8 12.5 all-to-all-start.3
  1285.3 11.1 fusion.4
  1296.4 18.1 %convert_bitcast_fusion = bf16[32,2,48,1536]{3,2,0,1:T(8,128)(2,1)} fusion(f32[2,32,48,512]{3,2,1,0:T(8,128)} %fusion.4, bf16[2,2,512,1536]{3,2,1,0:T(8,128)(2,1)} %param.11, bf16[32,2,48,1536]{3,2,1,0:T(8,128)(2,1)} %all-to-all-done.6, bf16[2,2,1536,512]{3,2,1,0:T(8,128)(2,1)} %param.9), kind=kOutput, calls=%fused_computation.16 | convolution fusion | flops 9677832192 | bytes 31457280 | tf_op jit(solution)/shard_map/dkcf,kfh->dkch/dot_general | solution.py:30
  1314.5 8.2 copy.137
  1322.7 160.8 %all-to-all-done.3 = bf16[32,2,48,1536]{3,2,1,0:T(8,128)(2,1)} async-done(((bf16[32,2,48,1536]{3,2,1,0:T(8,128)(2,1)}), bf16[32,2,48,1536]{3,2,1,0:T(8,128)(2,1)}, u32[]{:S(2)}, u32[]{:S(2)}) %all-to-all-start.3) | async-done | bytes 9437216 | tf_op jit(solution)/shard_map/all_to_all | solution.py:54
  1483.5 12.7 all-to-all-start.7
  1504.5 7.3 fusion.76
  1511.8 182.5 %all-to-all-done.7 = bf16[32,2,48,1536]{3,2,1,0:T(8,128)(2,1)} async-done(((bf16[32,2,48,1536]{3,2,1,0:T(8,128)(2,1)}), bf16[32,2,48,1536]{3,2,1,0:T(8,128)(2,1)}, u32[]{:S(2)}, u32[]{:S(2)}) %all-to-all-start.7) | async-done | bytes 9437216 | tf_op jit(solution)/shard_map/all_to_all | solution.py:54
  1694.3 6.3 fusion.77
  (63 shorter events, 62.0 us)
Async XLA Ops:
  12.4 13.0 copy-start
  12.4 205.7 %all-to-all-start = ((bf16[32,2,48,1536]{3,2,1,0:T(8,128)(2,1)}), bf16[32,2,48,1536]{3,2,1,0:T(8,128)(2,1)}, u32[]{:S(2)}, u32[]{:S(2)}) async-start(bf16[32,2,48,1536]{3,2,1,0:T(8,128)(2,1)} %bitcast.278), calls=%async_computation | async-start | bytes 18874368 | tf_op jit(solution)/shard_map/all_to_all | solution.py:52
  218.1 210.9 %all-to-all-start.4 = ((bf16[32,2,48,1536]{3,2,1,0:T(8,128)(2,1)}), bf16[32,2,48,1536]{3,2,1,0:T(8,128)(2,1)}, u32[]{:S(2)}, u32[]{:S(2)}) async-start(bf16[32,2,48,1536]{3,2,1,0:T(8,128)(2,1)} %bitcast.279), calls=%async_computation.4 | async-start | bytes 18874368 | tf_op jit(solution)/shard_map/all_to_all | solution.py:52
  429.0 211.0 %all-to-all-start.1 = ((bf16[32,2,48,1536]{3,2,1,0:T(8,128)(2,1)}), bf16[32,2,48,1536]{3,2,1,0:T(8,128)(2,1)}, u32[]{:S(2)}, u32[]{:S(2)}) async-start(bf16[32,2,48,1536]{3,2,1,0:T(8,128)(2,1)} %copy.116), calls=%async_computation.1 | async-start | bytes 18874368 | tf_op jit(solution)/shard_map/all_to_all | solution.py:54
  479.3 173.8 %copy-start.2 = (f32[2,2,256,6]{2,1,3,0:T(2,128)S(1)}, f32[2,2,256,6]{2,1,3,0:T(2,128)}, u32[]{:S(2)}) copy-start(f32[2,2,256,6]{2,1,3,0:T(2,128)} %param.8) | copy-start | bytes 73732
  640.0 211.2 %all-to-all-start.5 = ((bf16[32,2,48,1536]{3,2,1,0:T(8,128)(2,1)}), bf16[32,2,48,1536]{3,2,1,0:T(8,128)(2,1)}, u32[]{:S(2)}, u32[]{:S(2)}) async-start(bf16[32,2,48,1536]{3,2,1,0:T(8,128)(2,1)} %copy.130), calls=%async_computation.5 | async-start | bytes 18874368 | tf_op jit(solution)/shard_map/all_to_all | solution.py:54
  851.2 210.8 %all-to-all-start.2 = ((bf16[32,2,48,1536]{3,2,1,0:T(8,128)(2,1)}), bf16[32,2,48,1536]{3,2,1,0:T(8,128)(2,1)}, u32[]{:S(2)}, u32[]{:S(2)}) async-start(bf16[32,2,48,1536]{3,2,1,0:T(8,128)(2,1)} %bitcast.280), calls=%async_computation.2 | async-start | bytes 18874368 | tf_op jit(solution)/shard_map/all_to_all | solution.py:52
  1062.0 210.7 %all-to-all-start.6 = ((bf16[32,2,48,1536]{3,2,1,0:T(8,128)(2,1)}), bf16[32,2,48,1536]{3,2,1,0:T(8,128)(2,1)}, u32[]{:S(2)}, u32[]{:S(2)}) async-start(bf16[32,2,48,1536]{3,2,1,0:T(8,128)(2,1)} %bitcast.281), calls=%async_computation.6 | async-start | bytes 18874368 | tf_op jit(solution)/shard_map/all_to_all | solution.py:52
  1272.8 210.7 %all-to-all-start.3 = ((bf16[32,2,48,1536]{3,2,1,0:T(8,128)(2,1)}), bf16[32,2,48,1536]{3,2,1,0:T(8,128)(2,1)}, u32[]{:S(2)}, u32[]{:S(2)}) async-start(bf16[32,2,48,1536]{3,2,1,0:T(8,128)(2,1)} %copy.123), calls=%async_computation.3 | async-start | bytes 18874368 | tf_op jit(solution)/shard_map/all_to_all | solution.py:54
  1483.5 210.8 %all-to-all-start.7 = ((bf16[32,2,48,1536]{3,2,1,0:T(8,128)(2,1)}), bf16[32,2,48,1536]{3,2,1,0:T(8,128)(2,1)}, u32[]{:S(2)}, u32[]{:S(2)}) async-start(bf16[32,2,48,1536]{3,2,1,0:T(8,128)(2,1)} %copy.137), calls=%async_computation.7 | async-start | bytes 18874368 | tf_op jit(solution)/shard_map/all_to_all | solution.py:54
  1694.3 6.4 copy-start.1
where the time goes:
time: 1720 us; the launch traced here: 1700 us
  waiting for transfers between devices  1370 us (80%)
  matrix products  165 us (10%)
  starting transfers between devices  96.9 us (6%)
  other arithmetic  38.1 us (2%)
  local copies, waits for them, and re-layouts  34.5 us (2%)
    all_to_all x4, waiting for transfers between devices, device_body(): recv_buf = lax.all_to_all(send_buf, MESH_AXES, 0, 0, tiled=True)  686 us
    all_to_all x4, waiting for transfers between devices, device_body(): returned = lax.all_to_all(expert_out, MESH_AXES, 0, 0, tiled=True)  681 us
    dot_general x4, matrix products, expert_ffn(): jnp.einsum('dkcf,kfh->dkch', hidden, mat_down, preferred_element_type=jnp...  72.4 us
    all_to_all x4, starting transfers between devices, device_body(): returned = lax.all_to_all(expert_out, MESH_AXES, 0, 0, tiled=True)  51.2 us
    all_to_all x4, starting transfers between devices, device_body(): recv_buf = lax.all_to_all(send_buf, MESH_AXES, 0, 0, tiled=True)  45.6 us
    dot_general x4, matrix products, expert_ffn(): jnp.einsum('eldi,lig->eldg', expert_rows, mat_up3, preferred_element_type...  44.4 us
  transfers between devices with their start and end apart: 8, of which 8 were waited for; matrix products, arithmetic and copies ran while one was open for 13% of the time, Pallas kernels for 0%

commit v1 on v0

v1 whole, which is shorter than its diff:
```python
import functools

import jax
import jax.numpy as jnp
from jax import lax
from jax.experimental import pallas as pl
from jax.experimental.pallas import tpu as pltpu
from jax.sharding import PartitionSpec as P

ROUTE_SCALE = 2.5
MESH_AXES = ("ez", "ey", "ex")
PLANE_AXES = ("ey", "ex")


def capacity_of(tok_mb, top_k, experts):
    return 2 * ((tok_mb * top_k + experts - 1) // experts)


def slot_table(ids, experts, capacity):
    chosen = (ids[..., None] == jnp.arange(experts)).astype(jnp.int32)
    per_expert = jnp.sum(chosen, axis=-2)
    token_rank = jnp.cumsum(per_expert, axis=-2) - per_expert
    slot_pos = jnp.sum(chosen * token_rank[..., None, :], axis=-1)
    return ids * capacity + slot_pos


def dispatch_kernel(slots_ref, tok_ref, out_ref):
    block = out_ref.shape[2]
    top_k, tok_mb = slots_ref.shape[1:]
    row = lax.broadcasted_iota(jnp.int32, (block, tok_mb), 0) + pl.program_id(1) * block
    hit = jnp.zeros((block, tok_mb), jnp.bool_)
    for k in range(top_k):
        hit = hit | (slots_ref[0, k:k + 1, :] == row)
    pick = jnp.where(hit, 1.0, 0.0).astype(jnp.bfloat16)
    out_ref[0, 0] = jnp.dot(pick, tok_ref[0], preferred_element_type=jnp.float32).astype(jnp.bfloat16)


def dispatch(slots_t, tokens, plane, block):
    n_src, tok_mb, hidden = tokens.shape
    top_k = slots_t.shape[1]
    return pl.pallas_call(
        dispatch_kernel,
        grid=(n_src, plane),
        in_specs=[
            pl.BlockSpec((1, top_k, tok_mb), lambda s, p: (s, 0, 0)),
            pl.BlockSpec((1, tok_mb, hidden), lambda s, p: (s, 0, 0)),
        ],
        out_specs=pl.BlockSpec((1, 1, block, hidden), lambda s, p: (p, s, 0, 0)),
        out_shape=jax.ShapeDtypeStruct((plane, n_src, block, hidden), jnp.bfloat16),
        cost_estimate=pl.CostEstimate(flops=2 * n_src * plane * block * tok_mb * hidden, bytes_accessed=n_src * plane * block * hidden * 2, transcendentals=0),
    )(slots_t, tokens)


def combine_kernel(slots_ref, gates_ref, rows_ref, out_ref):
    block = rows_ref.shape[2]
    tok_mb, top_k = slots_ref.shape[1:]
    p = pl.program_id(1)
    col = lax.broadcasted_iota(jnp.int32, (tok_mb, block), 1) + p * block
    weight = jnp.zeros((tok_mb, block), jnp.float32)
    for k in range(top_k):
        weight = weight + jnp.where(slots_ref[0, :, k:k + 1] == col, gates_ref[0, :, k:k + 1], 0.0)
    high = weight.astype(jnp.bfloat16)
    low = (weight - high.astype(jnp.float32)).astype(jnp.bfloat16)
    rows = rows_ref[0, 0]
    part = jnp.dot(high, rows, preferred_element_type=jnp.float32) + jnp.dot(low, rows, preferred_element_type=jnp.float32)

    @pl.when(p == 0)
    def _():
        out_ref[0] = part

    @pl.when(p != 0)
    def _():
        out_ref[0] += part


def combine(slots, gates, rows):
    plane, n_src, block, hidden = rows.shape
    tok_mb, top_k = slots.shape[1:]
    return pl.pallas_call(
        combine_kernel,
        grid=(n_src, plane),
        in_specs=[
            pl.BlockSpec((1, tok_mb, top_k), lambda s, p: (s, 0, 0)),
            pl.BlockSpec((1, tok_mb, top_k), lambda s, p: (s, 0, 0)),
            pl.BlockSpec((1, 1, block, hidden), lambda s, p: (p, s, 0, 0)),
        ],
        out_specs=pl.BlockSpec((1, tok_mb, hidden), lambda s, p: (s, 0, 0)),
        out_shape=jax.ShapeDtypeStruct((n_src, tok_mb, hidden), jnp.float32),
        cost_estimate=pl.CostEstimate(flops=4 * n_src * plane * block * tok_mb * hidden, bytes_accessed=n_src * plane * block * hidden * 4, transcendentals=0),
    )(slots, gates, rows)


def expert_ffn(rows, mat_up1, mat_up3, mat_down):
    gate_in = jnp.einsum("pseci,eig->psecg", rows, mat_up1, preferred_element_type=jnp.float32)
    lin_in = jnp.einsum("pseci,eig->psecg", rows, mat_up3, preferred_element_type=jnp.float32)
    hidden = (jax.nn.silu(gate_in) * lin_in).astype(jnp.bfloat16)
    return jnp.einsum("psecf,efh->psech", hidden, mat_down, preferred_element_type=jnp.float32).astype(jnp.bfloat16)


def solution(mesh):
    n_z = mesh.shape["ez"]
    plane = mesh.shape["ey"] * mesh.shape["ex"]
    n_dev = n_z * plane
    tok_spec = P(None, MESH_AXES, None)
    route_spec = P(None, None, MESH_AXES, None)
    weight_spec = P(None, MESH_AXES, None, None)

    def device_body(tokens_in, expert_ids, gate_vals, w_up1, w_up3, w_down):
        n_layers, n_micro, tok_mb, top_k = expert_ids.shape
        exp_dev = w_up1.shape[1]
        hidden_size = tokens_in.shape[-1]
        experts = exp_dev * n_dev
        capacity = capacity_of(tok_mb, top_k, experts)
        block = exp_dev * capacity
        slots = slot_table(expert_ids, experts, capacity)
        routes = jnp.concatenate([slots.astype(jnp.float32), gate_vals], axis=-1)
        routes = lax.all_gather(routes, "ez", axis=2)
        first_slot = lax.axis_index("ez") * (plane * block)
        slots = routes[..., :top_k].astype(jnp.int32) - first_slot
        gates = routes[..., top_k:]
        slots_t = jnp.swapaxes(slots, -1, -2)
        batches = [tokens_in[mb] for mb in range(n_micro)]
        for layer in range(n_layers):
            for mb in range(n_micro):
                tokens = batches[mb]
                column = lax.all_gather(tokens, "ez", axis=0)
                send = dispatch(slots_t[layer, mb], column, plane, block)
                recv = lax.all_to_all(send, PLANE_AXES, 0, 0, tiled=True)
                recv = recv.reshape(plane, n_z, exp_dev, capacity, hidden_size)
                out = expert_ffn(recv, w_up1[layer], w_up3[layer], w_down[layer])
                back = lax.all_to_all(out.reshape(plane, n_z, block, hidden_size), PLANE_AXES, 0, 0, tiled=True)
                part = combine(slots[layer, mb], gates[layer, mb], back)
                moe_sum = lax.psum_scatter(part, "ez", scatter_dimension=0, tiled=False)
                batches[mb] = (tokens.astype(jnp.float32) + ROUTE_SCALE * moe_sum).astype(jnp.bfloat16)
        return jnp.stack(batches)

    return jax.shard_map(device_body, mesh=mesh, in_specs=(tok_spec, route_spec, route_spec, weight_spec, weight_spec, weight_spec), out_specs=tok_spec, check_vma=False)
```

time: 1720 us -> 1530 us (0.89)
  waiting for transfers between devices: 1370 us -> 805 us
  Pallas kernels: 0 us -> 247 us
  blocking collectives: 0 us -> 240 us
  starting transfers between devices: 96.9 us -> 31.3 us
  matrix products: 165 us -> 117 us
  other arithmetic: 38.1 us -> 11.5 us
    all_to_all x8 -> x6, waiting for transfers between devices: 1370 us -> 362 us  [the longest x2 184 us: device_body(): lax.all_to_all(out.reshape(plane, n_z, block, hidden_size), PLANE_AXES, 0...]
    pallas_call x0 -> x8, Pallas kernels: none -> 247 us  [the longest x4 169 us: combine(): pl.pallas_call(combine_kernel, grid=(n_src, plane), in_specs=[pl.BlockSpe...]
    all_gather x0 -> x4, waiting for transfers between devices: none -> 229 us  [device_body(): column = lax.all_gather(tokens, 'ez', axis=0)]
    all_to_all x0 -> x2, blocking collectives: none -> 222 us  [device_body(): lax.all_to_all(out.reshape(plane, n_z, block, hidden_size), PLANE_AXES, 0...]
    reduce_scatter x0 -> x4, waiting for transfers between devices: none -> 213 us  [device_body(): moe_sum = lax.psum_scatter(part, 'ez', scatter_dimension=0, tiled=False)]
    all_to_all x8 -> x6, starting transfers between devices: 96.9 us -> 30.6 us  [the longest x4 20.5 us: device_body(): recv = lax.all_to_all(send, PLANE_AXES, 0, 0, tiled=True)]
    dot_general x16 -> x8, matrix products: 165 us -> 117 us  [the longest x4 72.9 us: expert_ffn(): jnp.einsum('psecf,efh->psech', hidden, mat_down, preferred_element_type=j...]
    all_gather x0 -> x1, blocking collectives: none -> 17.9 us  [device_body(): routes = lax.all_gather(routes, 'ez', axis=2)]
  transfers between devices with their start and end apart: 8 -> 14, of which waited for: 8 -> 12; matrix products, arithmetic and copies ran while one was open for 13% -> 11% of each run, Pallas kernels for 0% -> 8%
where the time goes in v1:
time: 1530 us; the launch traced here: 1520 us
  waiting for transfers between devices  805 us (53%)
  Pallas kernels  247 us (16%)
  blocking collectives  240 us (16%)
  matrix products  117 us (8%)
  local copies, waits for them, and re-layouts  50.1 us (3%)
  starting transfers between devices  31.3 us (2%)
    all_gather x4, waiting for transfers between devices, device_body(): column = lax.all_gather(tokens, 'ez', axis=0)  229 us
    all_to_all x2, blocking collectives, device_body(): lax.all_to_all(out.reshape(plane, n_z, block, hidden_size), PLANE_AXES, 0...  222 us
    reduce_scatter x4, waiting for transfers between devices, device_body(): moe_sum = lax.psum_scatter(part, 'ez', scatter_dimension=0, tiled=False)  213 us
    all_to_all x2, waiting for transfers between devices, device_body(): lax.all_to_all(out.reshape(plane, n_z, block, hidden_size), PLANE_AXES, 0...  184 us
    all_to_all x4, waiting for transfers between devices, device_body(): recv = lax.all_to_all(send, PLANE_AXES, 0, 0, tiled=True)  178 us
    pallas_call x4, Pallas kernels, combine(): pl.pallas_call(combine_kernel, grid=(n_src, plane), in_specs=[pl.BlockSpe...  169 us
    pallas_call x4, Pallas kernels, dispatch(): pl.pallas_call(dispatch_kernel, grid=(n_src, plane), in_specs=[pl.BlockSp...  77.8 us
    dot_general x4, matrix products, expert_ffn(): jnp.einsum('psecf,efh->psech', hidden, mat_down, preferred_element_type=j...  72.9 us
  transfers between devices with their start and end apart: 14, of which 12 were waited for; matrix products, arithmetic and copies ran while one was open for 11% of the time, Pallas kernels for 8%

profile of v1, /device:TPU:0, one launch (start us, length us, event | category | flops | bytes accessed | tf_op | source)
XLA Modules:
  0.0 1516.2 jit_solution(1504950138191942563)
XLA Ops:
  14.1 17.9 %all-gather = f32[2,2,1024,12]{2,3,1,0:T(8,128)S(1)} all-gather(f32[2,2,256,12]{2,3,1,0:T(8,128)S(1)} %pad_maximum_fusion.1), channel_id=2, replica_groups=mesh['ez'=4,'ey'=2,'ex'=4] {'ez'}, dimensions={2}, use_global_device_ids=true | all-gather | bytes 245760 | tf_op jit(solution)/shard_map/all_gather | solution.py:117
  36.0 41.5 %all-gather.10.cloned.1.call-done.tok_ref = bf16[4,256,1536]{2,1,0:T(8,128)(2,1)} async-done(((bf16[1,256,1536]{2,1,0:T(8,128)(2,1)}), bf16[4,256,1536]{2,1,0:T(8,128)(2,1)}) %all-gather.10.cloned.1.call-update) | async-done | bytes 3145744 | tf_op jit(solution)/shard_map/all_gather | solution.py:126
  77.5 19.5 %shard_map.68 = bf16[8,4,96,1536]{3,2,1,0:T(8,128)(2,1)} custom-call(s32[4,6,256]{2,1,0:T(8,128)} %copy.73.slots_ref, bf16[4,256,1536]{2,1,0:T(8,128)(2,1)} %all-gather.10.cloned.1.call-done.tok_ref), custom_call_target="tpu_custom_call" | custom-call | flops 2415919104 | bytes 9437184 | tf_op jit(solution)/shard_map/pallas_call | solution.py:41
  104.6 62.3 %all-gather.6.cloned.1.call-done.tok_ref = bf16[4,256,1536]{2,1,0:T(8,128)(2,1)} async-done(((bf16[1,256,1536]{2,1,0:T(8,128)(2,1)}), bf16[4,256,1536]{2,1,0:T(8,128)(2,1)}) %all-gather.6.cloned.1.call-update) | async-done | bytes 3145744 | tf_op jit(solution)/shard_map/all_gather | solution.py:126
  166.9 19.5 %shard_map.64 = bf16[8,4,96,1536]{3,2,1,0:T(8,128)(2,1)} custom-call(s32[4,6,256]{2,1,0:T(8,128)} %copy.65.slots_ref, bf16[4,256,1536]{2,1,0:T(8,128)(2,1)} %all-gather.6.cloned.1.call-done.tok_ref), custom_call_target="tpu_custom_call" | custom-call | flops 2415919104 | bytes 9437184 | tf_op jit(solution)/shard_map/pallas_call | solution.py:41
  186.4 20.9 %all-to-all-done.4 = bf16[8,4,96,1536]{3,2,1,0:T(8,128)(2,1)} async-done(((bf16[8,4,96,1536]{3,2,1,0:T(8,128)(2,1)}), bf16[8,4,96,1536]{3,2,1,0:T(8,128)(2,1)}, u32[]{:S(2)}, u32[]{:S(2)}) %all-to-all-start.4) | async-done | bytes 9437216 | tf_op jit(solution)/shard_map/all_to_all | solution.py:128
  212.4 11.1 fusion.4
  223.4 18.1 %convert_bitcast_fusion.1 = bf16[8,4,2,48,1536]{4,3,1,0,2:T(8,128)(2,1)} fusion(f32[2,8,4,48,512]{4,3,2,1,0:T(8,128)} %fusion.4, bf16[8,4,2,48,1536]{4,3,2,1,0:T(8,128)(2,1)} %bitcast.41, bf16[2,2,512,1536]{3,2,1,0:T(8,128)(2,1)} %param.11, bf16[2,2,1536,512]{3,2,1,0:T(8,128)(2,1)} %param.9), kind=kOutput, calls=%fused_computation.1 | convolution fusion | flops 9677832192 | bytes 31457280 | tf_op jit(solution)/shard_map/psecf,efh->psech/dot_general | solution.py:97
  249.8 67.8 %all-to-all-done = bf16[8,4,96,1536]{3,2,1,0:T(8,128)(2,1)} async-done(((bf16[8,4,96,1536]{3,2,1,0:T(8,128)(2,1)}), bf16[8,4,96,1536]{3,2,1,0:T(8,128)(2,1)}, u32[]{:S(2)}, u32[]{:S(2)}) %all-to-all-start) | async-done | bytes 9437216 | tf_op jit(solution)/shard_map/all_to_all | solution.py:128
  327.5 10.7 fusion.12
  338.2 89.7 %all-to-all-done.5.rows_ref = bf16[8,4,96,1536]{3,2,1,0:T(8,128)(2,1)} async-done(((bf16[8,4,96,1536]{3,2,1,0:T(8,128)(2,1)}), bf16[8,4,96,1536]{3,2,1,0:T(8,128)(2,1)}, u32[]{:S(2)}, u32[]{:S(2)}) %all-to-all-start.5) | async-done | bytes 9437216 | tf_op jit(solution)/shard_map/all_to_all | solution.py:131
  427.9 42.3 %shard_map.69 = f32[4,256,1536]{2,1,0:T(8,128)} custom-call(s32[4,256,6]{2,1,0:T(8,128)} %get-tuple-element.15.slots_ref, f32[4,256,6]{2,1,0:T(8,128)} %get-tuple-element.11.gates_ref, bf16[8,4,96,1536]{3,2,1,0:T(8,128)(2,1)} %all-to-all-done.5.rows_ref), custom_call_target="tpu_custom_call" | custom-call | flops 4831838208 | bytes 18874368 | tf_op jit(solution)/shard_map/pallas_call | solution.py:79
  470.3 18.2 %convert_bitcast_fusion.3 = bf16[8,4,2,48,1536]{4,3,1,0,2:T(8,128)(2,1)} fusion(f32[2,8,4,48,512]{4,3,2,1,0:T(8,128)} %fusion.12, bf16[8,4,2,48,1536]{4,3,2,1,0:T(8,128)(2,1)} %bitcast.7, bf16[2,2,512,1536]{3,2,1,0:T(8,128)(2,1)} %param.11, bf16[2,2,1536,512]{3,2,1,0:T(8,128)(2,1)} %param.9), kind=kOutput, calls=%fused_computation.3 | convolution fusion | flops 9677832192 | bytes 31457280 | tf_op jit(solution)/shard_map/psecf,efh->psech/dot_general | solution.py:97
  488.5 8.3 copy.68
  496.8 110.9 %all_to_all.40.rows_ref = bf16[8,4,96,1536]{3,2,1,0:T(8,128)(2,1)} all-to-all(bf16[8,4,96,1536]{3,2,1,0:T(8,128)(2,1)} %bitcast.196), channel_id=1, replica_groups=mesh['ez'=4,'ey'=2,'ex'=4] {'ey','ex'}, dimensions={0} | all-to-all | bytes 18874368 | tf_op jit(solution)/shard_map/all_to_all | solution.py:131
  607.7 42.3 %shard_map.65 = f32[4,256,1536]{2,1,0:T(8,128)} custom-call(s32[4,256,6]{2,1,0:T(8,128)} %get-tuple-element.13.slots_ref, f32[4,256,6]{2,1,0:T(8,128)} %get-tuple-element.9.gates_ref, bf16[8,4,96,1536]{3,2,1,0:T(8,128)(2,1)} %all_to_all.40.rows_ref), custom_call_target="tpu_custom_call" | custom-call | flops 4831838208 | bytes 18874368 | tf_op jit(solution)/shard_map/pallas_call | solution.py:79
  650.1 108.0 %reduce-scatter.5.cloned.1.call-done = f32[1,256,1536]{2,1,0:T(8,128)} async-done(((f32[4,256,1536]{2,1,0:T(8,128)}), f32[1,256,1536]{2,1,0:T(8,128)}) %reduce-scatter.5.cloned.1.call-update) | async-done | bytes 1572880 | tf_op jit(solution)/shard_map/reduce_scatter | solution.py:133
  762.5 62.8 %all-gather.8.cloned.1.call-done.tok_ref = bf16[4,256,1536]{2,1,0:T(8,128)(2,1)} async-done(((bf16[1,256,1536]{2,1,0:T(8,128)(2,1)}), bf16[4,256,1536]{2,1,0:T(8,128)(2,1)}) %all-gather.8.cloned.1.call-update) | async-done | bytes 3145744 | tf_op jit(solution)/shard_map/all_gather | solution.py:126
  825.3 19.5 %shard_map.66 = bf16[8,4,96,1536]{3,2,1,0:T(8,128)(2,1)} custom-call(s32[4,6,256]{2,1,0:T(8,128)} %copy.69.slots_ref, bf16[4,256,1536]{2,1,0:T(8,128)(2,1)} %all-gather.8.cloned.1.call-done.tok_ref), custom_call_target="tpu_custom_call" | custom-call | flops 2415919104 | bytes 9437184 | tf_op jit(solution)/shard_map/pallas_call | solution.py:41
  851.2 62.8 %all-gather.12.cloned.1.call-done.tok_ref = bf16[4,256,1536]{2,1,0:T(8,128)(2,1)} async-done(((bf16[1,256,1536]{2,1,0:T(8,128)(2,1)}), bf16[4,256,1536]{2,1,0:T(8,128)(2,1)}) %all-gather.12.cloned.1.call-update) | async-done | bytes 3145744 | tf_op jit(solution)/shard_map/all_gather | solution.py:126
  914.0 19.4 %shard_map.70 = bf16[8,4,96,1536]{3,2,1,0:T(8,128)(2,1)} custom-call(s32[4,6,256]{2,1,0:T(8,128)} %copy.77.slots_ref, bf16[4,256,1536]{2,1,0:T(8,128)(2,1)} %all-gather.12.cloned.1.call-done.tok_ref), custom_call_target="tpu_custom_call" | custom-call | flops 2415919104 | bytes 9437184 | tf_op jit(solution)/shard_map/pallas_call | solution.py:41
  933.4 21.7 %all-to-all-done.2 = bf16[8,4,96,1536]{3,2,1,0:T(8,128)(2,1)} async-done(((bf16[8,4,96,1536]{3,2,1,0:T(8,128)(2,1)}), bf16[8,4,96,1536]{3,2,1,0:T(8,128)(2,1)}, u32[]{:S(2)}, u32[]{:S(2)}) %all-to-all-start.2) | async-done | bytes 9437216 | tf_op jit(solution)/shard_map/all_to_all | solution.py:128
  960.3 11.2 fusion.8
  971.5 18.2 %convert_bitcast_fusion.2 = bf16[8,4,2,48,1536]{4,3,1,0,2:T(8,128)(2,1)} fusion(f32[2,8,4,48,512]{4,3,2,1,0:T(8,128)} %fusion.8, bf16[8,4,2,48,1536]{4,3,2,1,0:T(8,128)(2,1)} %bitcast.24, bf16[2,2,512,1536]{3,2,1,0:T(8,128)(2,1)} %param.11, bf16[2,2,1536,512]{3,2,1,0:T(8,128)(2,1)} %param.9), kind=kOutput, calls=%fused_computation.2 | convolution fusion | flops 9677832192 | bytes 31457280 | tf_op jit(solution)/shard_map/psecf,efh->psech/dot_general | solution.py:97
  998.0 67.5 %all-to-all-done.6 = bf16[8,4,96,1536]{3,2,1,0:T(8,128)(2,1)} async-done(((bf16[8,4,96,1536]{3,2,1,0:T(8,128)(2,1)}), bf16[8,4,96,1536]{3,2,1,0:T(8,128)(2,1)}, u32[]{:S(2)}, u32[]{:S(2)}) %all-to-all-start.6) | async-done | bytes 9437216 | tf_op jit(solution)/shard_map/all_to_all | solution.py:128
  1070.7 11.1 fusion
  1081.8 94.1 %all-to-all-done.3.rows_ref = bf16[8,4,96,1536]{3,2,1,0:T(8,128)(2,1)} async-done(((bf16[8,4,96,1536]{3,2,1,0:T(8,128)(2,1)}), bf16[8,4,96,1536]{3,2,1,0:T(8,128)(2,1)}, u32[]{:S(2)}, u32[]{:S(2)}) %all-to-all-start.3) | async-done | bytes 9437216 | tf_op jit(solution)/shard_map/all_to_all | solution.py:131
  1175.9 42.3 %shard_map.67 = f32[4,256,1536]{2,1,0:T(8,128)} custom-call(s32[4,256,6]{2,1,0:T(8,128)} %get-tuple-element.16.slots_ref, f32[4,256,6]{2,1,0:T(8,128)} %get-tuple-element.12.gates_ref, bf16[8,4,96,1536]{3,2,1,0:T(8,128)(2,1)} %all-to-all-done.3.rows_ref), custom_call_target="tpu_custom_call" | custom-call | flops 4831838208 | bytes 18874368 | tf_op jit(solution)/shard_map/pallas_call | solution.py:79
  1218.6 18.2 %convert_bitcast_fusion = bf16[8,4,2,48,1536]{4,3,1,0,2:T(8,128)(2,1)} fusion(f32[2,8,4,48,512]{4,3,2,1,0:T(8,128)} %fusion, bf16[8,4,2,48,1536]{4,3,2,1,0:T(8,128)(2,1)} %bitcast.55, bf16[2,2,512,1536]{3,2,1,0:T(8,128)(2,1)} %param.11, bf16[2,2,1536,512]{3,2,1,0:T(8,128)(2,1)} %param.9), kind=kOutput, calls=%fused_computation | convolution fusion | flops 9677832192 | bytes 31457280 | tf_op jit(solution)/shard_map/psecf,efh->psech/dot_general | solution.py:97
  1245.1 110.9 %all_to_all.41.rows_ref = bf16[8,4,96,1536]{3,2,1,0:T(8,128)(2,1)} all-to-all(bf16[8,4,96,1536]{3,2,1,0:T(8,128)(2,1)} %bitcast.197), channel_id=1, replica_groups=mesh['ez'=4,'ey'=2,'ex'=4] {'ey','ex'}, dimensions={0} | all-to-all | bytes 18874368 | tf_op jit(solution)/shard_map/all_to_all | solution.py:131
  1356.0 42.3 %shard_map.71 = f32[4,256,1536]{2,1,0:T(8,128)} custom-call(s32[4,256,6]{2,1,0:T(8,128)} %get-tuple-element.14.slots_ref, f32[4,256,6]{2,1,0:T(8,128)} %get-tuple-element.10.gates_ref, bf16[8,4,96,1536]{3,2,1,0:T(8,128)(2,1)} %all_to_all.41.rows_ref), custom_call_target="tpu_custom_call" | custom-call | flops 4831838208 | bytes 18874368 | tf_op jit(solution)/shard_map/pallas_call | solution.py:79
  1401.0 105.0 %reduce-scatter.11.cloned.1.call-done = f32[1,256,1536]{2,1,0:T(8,128)} async-done(((f32[4,256,1536]{2,1,0:T(8,128)}), f32[1,256,1536]{2,1,0:T(8,128)}) %reduce-scatter.11.cloned.1.call-update) | async-done | bytes 1572880 | tf_op jit(solution)/shard_map/reduce_scatter | solution.py:133
  (67 shorter events, 86.0 us)
Async XLA Ops:
  6.5 7.6 copy-start.3
  6.5 71.0 %all-gather.10.cloned.1.call-start = ((), (), s32[]{:S(2)}) async-start(), calls=%async_computation.16 | async-start | bytes 3932160 | tf_op jit(solution)/shard_map/all_gather | solution.py:126
  97.0 110.3 %all-to-all-start.4 = ((bf16[8,4,96,1536]{3,2,1,0:T(8,128)(2,1)}), bf16[8,4,96,1536]{3,2,1,0:T(8,128)(2,1)}, u32[]{:S(2)}, u32[]{:S(2)}) async-start(bf16[8,4,96,1536]{3,2,1,0:T(8,128)(2,1)} %shard_map.68), calls=%async_computation.6 | async-start | bytes 18874368 | tf_op jit(solution)/shard_map/all_to_all | solution.py:128
  102.1 64.8 %all-gather.6.cloned.1.call-start = ((), (), s32[]{:S(2)}) async-start(), calls=%async_computation.12 | async-start | bytes 3932160 | tf_op jit(solution)/shard_map/all_gather | solution.py:126
  207.3 110.3 %all-to-all-start = ((bf16[8,4,96,1536]{3,2,1,0:T(8,128)(2,1)}), bf16[8,4,96,1536]{3,2,1,0:T(8,128)(2,1)}, u32[]{:S(2)}, u32[]{:S(2)}) async-start(bf16[8,4,96,1536]{3,2,1,0:T(8,128)(2,1)} %shard_map.64), calls=%async_computation | async-start | bytes 18874368 | tf_op jit(solution)/shard_map/all_to_all | solution.py:128
  317.6 110.3 %all-to-all-start.5 = ((bf16[8,4,96,1536]{3,2,1,0:T(8,128)(2,1)}), bf16[8,4,96,1536]{3,2,1,0:T(8,128)(2,1)}, u32[]{:S(2)}, u32[]{:S(2)}) async-start(bf16[8,4,96,1536]{3,2,1,0:T(8,128)(2,1)} %bitcast.194), calls=%async_computation.7 | async-start | bytes 18874368 | tf_op jit(solution)/shard_map/all_to_all | solution.py:131
  322.6 327.5 %reduce-scatter.9.cloned.1.call-start = ((), (), s32[]{:S(2)}) async-start(), calls=%async_computation.17 | async-start | bytes 7864320 | tf_op jit(solution)/shard_map/reduce_scatter | solution.py:133
  322.9 3.6 slice-start
  324.8 2.7 slice-start.1
  470.2 287.9 %reduce-scatter.5.cloned.1.call-start = ((), (), s32[]{:S(2)}) async-start(), calls=%async_computation.13 | async-start | bytes 7864320 | tf_op jit(solution)/shard_map/reduce_scatter | solution.py:133
  650.0 108.2 %copy-start.2 = (bf16[2,256,1536]{2,1,0:T(8,128)(2,1)S(1)}, bf16[2,256,1536]{2,1,0:T(8,128)(2,1)}, u32[]{:S(2)}) copy-start(bf16[2,256,1536]{2,1,0:T(8,128)(2,1)} %param.6) | copy-start | bytes 4718596
  650.0 175.3 %all-gather.8.cloned.1.call-start = ((), (), s32[]{:S(2)}) async-start(), calls=%async_computation.14 | async-start | bytes 3932160 | tf_op jit(solution)/shard_map/all_gather | solution.py:126
  844.8 110.3 %all-to-all-start.2 = ((bf16[8,4,96,1536]{3,2,1,0:T(8,128)(2,1)}), bf16[8,4,96,1536]{3,2,1,0:T(8,128)(2,1)}, u32[]{:S(2)}, u32[]{:S(2)}) async-start(bf16[8,4,96,1536]{3,2,1,0:T(8,128)(2,1)} %shard_map.66), calls=%async_computation.3 | async-start | bytes 18874368 | tf_op jit(solution)/shard_map/all_to_all | solution.py:128
  849.8 64.2 %all-gather.12.cloned.1.call-start = ((), (), s32[]{:S(2)}) async-start(), calls=%async_computation.18 | async-start | bytes 3932160 | tf_op jit(solution)/shard_map/all_gather | solution.py:126
  955.1 110.5 %all-to-all-start.6 = ((bf16[8,4,96,1536]{3,2,1,0:T(8,128)(2,1)}), bf16[8,4,96,1536]{3,2,1,0:T(8,128)(2,1)}, u32[]{:S(2)}, u32[]{:S(2)}) async-start(bf16[8,4,96,1536]{3,2,1,0:T(8,128)(2,1)} %shard_map.70), calls=%async_computation.9 | async-start | bytes 18874368 | tf_op jit(solution)/shard_map/all_to_all | solution.py:128
  1065.6 110.3 %all-to-all-start.3 = ((bf16[8,4,96,1536]{3,2,1,0:T(8,128)(2,1)}), bf16[8,4,96,1536]{3,2,1,0:T(8,128)(2,1)}, u32[]{:S(2)}, u32[]{:S(2)}) async-start(bf16[8,4,96,1536]{3,2,1,0:T(8,128)(2,1)} %bitcast.195), calls=%async_computation.4 | async-start | bytes 18874368 | tf_op jit(solution)/shard_map/all_to_all | solution.py:131
  1070.7 327.7 %reduce-scatter.7.cloned.1.call-start = ((), (), s32[]{:S(2)}) async-start(), calls=%async_computation.15 | async-start | bytes 7864320 | tf_op jit(solution)/shard_map/reduce_scatter | solution.py:133
  1218.3 287.8 %reduce-scatter.11.cloned.1.call-start = ((), (), s32[]{:S(2)}) async-start(), calls=%async_computation.19 | async-start | bytes 7864320 | tf_op jit(solution)/shard_map/reduce_scatter | solution.py:133
  1398.3 1.1 copy-start.1
  1398.3 107.8 %copy-start = (bf16[1,256,1536]{2,1,0:T(8,128)(2,1)S(1)}, bf16[1,256,1536]{2,1,0:T(8,128)(2,1)}, u32[]{:S(2)}) copy-start(bf16[1,256,1536]{2,1,0:T(8,128)(2,1)} %get-tuple-element.18) | copy-start | bytes 2359300
Sparse Core Ops, SparseCore 0:
  9.3 68.1 all-gather.9
  104.4 62.4 all-gather.5
  470.4 107.9 reduce-scatter.8
  650.2 107.9 reduce-scatter.4
  761.8 63.4 all-gather.7
  851.9 62.0 all-gather.11
  1218.4 107.5 reduce-scatter.6
  1398.4 107.5 reduce-scatter.10

commit v2 on v0

v2 whole, which is shorter than its diff:
```python
import functools

import jax
import jax.numpy as jnp
from jax import lax
from jax.experimental import pallas as pl
from jax.experimental.pallas import tpu as pltpu
from jax.sharding import PartitionSpec as P

ROUTE_SCALE = 2.5
MESH_AXES = ("ez", "ey", "ex")
N_Z = 4
N_PEER = 4
SEND_SLOTS = 3
VMEM_LIMIT = 67043328
COLUMN = 512


def capacity_of(tok_mb, top_k, experts):
    return 2 * ((tok_mb * top_k + experts - 1) // experts)


def slot_table(ids, experts, capacity):
    chosen = (ids[..., None] == jnp.arange(experts)).astype(jnp.int32)
    per_expert = jnp.sum(chosen, axis=-2)
    token_rank = jnp.cumsum(per_expert, axis=-2) - per_expert
    slot_pos = jnp.sum(chosen * token_rank[..., None, :], axis=-1)
    return ids * capacity + slot_pos


def moe_kernel(capacity, tok_in, slots_row, slots_col, gates_col, w_up1, w_up3, w_down,
               out, d_land, r_land, c_land, x_up1, x_up3, x_down,
               col, d_buf, r_buf, part, v_up1, v_up3, v_down, stage, sum_stage, w_hi, w_lo,
               ag_send, ag_recv, d_send, d_recv, r_send, r_recv, c_send, c_recv, x_send, x_recv, load_sem, copy_sem, self_sem):
    n_layers, n_micro = slots_row.shape[:2]
    top_k, tok_mb = slots_row.shape[3:]
    hidden = col.shape[-1]
    exp_dev = w_up1.shape[1]
    block = d_buf.shape[2]
    column = min(COLUMN, hidden)
    iz, iy, ie = lax.axis_index("ez"), lax.axis_index("ey"), lax.axis_index("ex")
    ix, ic = ie // 2, ie % 2
    edge = jnp.minimum(iz, N_Z - 1 - iz)
    low = iz < N_Z // 2
    is_end = edge == 0
    is_mid = edge == 1
    mesh_id = pl.DeviceIdType.MESH

    def peer_chip(r):
        return (iy + r // 2) % 2, (ix + r % 2) % 2

    def peer(r):
        py, px = peer_chip(r)
        return (iz, py, px * 2 + ic)

    def along_z(z):
        return (z, iy, ie)

    partner = (iz, iy, ix * 2 + (1 - ic))
    inner_z = jnp.where(low, jnp.where(is_end, 1, 2), jnp.where(is_end, 2, 1))
    outer_z = jnp.where(low, 0, N_Z - 1)

    def row_of(k):
        pos = jnp.where(k == 0, 3, jnp.where(k == 1, 2, jnp.where(k == 2, 1 - edge, edge)))
        return jnp.where(low, pos, N_Z - 1 - pos)

    barrier = pltpu.get_barrier_semaphore()
    for r in range(1, N_PEER):
        pl.semaphore_signal(barrier, inc=1, device_id=peer(r), device_id_type=mesh_id)
    for t in range(1, N_Z):
        pl.semaphore_signal(barrier, inc=1, device_id=along_z((iz + t) % N_Z), device_id_type=mesh_id)
    pl.semaphore_signal(barrier, inc=1, device_id=partner, device_id_type=mesh_id)
    pl.semaphore_wait(barrier, N_PEER + N_Z - 1)

    def remote(src, dst, send_sem, recv_sem, device):
        return pltpu.make_async_remote_copy(src_ref=src, dst_ref=dst, send_sem=send_sem, recv_sem=recv_sem, device_id=device, device_id_type=mesh_id)

    def gather_copy(m, t):
        return remote(col.at[m, iz], col.at[m, iz], ag_send.at[m, t - 1], ag_recv.at[m, iz], along_z((iz + t) % N_Z))

    def gather_start(m):
        for t in (2, 1, 3):
            gather_copy(m, t).start()

    def gather_sent(m):
        for t in range(1, N_Z):
            gather_copy(m, t).wait_send()

    def gather_wait(m, s):
        remote(col.at[m, s], col.at[m, s], ag_send.at[m, 0], ag_recv.at[m, s], partner).wait_recv()

    def d_copy(m, s, slot, r):
        if r == 0:
            return pltpu.make_async_copy(d_buf.at[slot, 0], d_land.at[m, s, 0], self_sem)
        return remote(d_buf.at[slot, r], d_land.at[m, s, r], d_send.at[slot, r], d_recv.at[m, s, r], peer(r))

    def r_copy(m, s, slot, r):
        if r == 0:
            return pltpu.make_async_copy(r_buf.at[slot, 0], r_land.at[m, s, 0], self_sem)
        return remote(r_buf.at[slot, r], r_land.at[m, s, r], r_send.at[slot, r], r_recv.at[m, s, r], peer(r))

    def buffer_free(copy, m, s, count):
        @pl.when(count >= SEND_SLOTS)
        def _():
            for r in range(1, N_PEER):
                copy(m, s, count % SEND_SLOTS, r).wait_send()

    def dispatch(l, m, s, count):
        slot = count % SEND_SLOTS
        buffer_free(d_copy, m, s, count)
        tokens = col[m, s]
        picks = slots_row[l, m, s]
        for r in range(N_PEER):
            py, px = peer_chip(r)
            row = lax.broadcasted_iota(jnp.int32, (block, tok_mb), 0) + (py * 2 + px) * block
            hit = jnp.zeros((block, tok_mb), jnp.bool_)
            for k in range(top_k):
                hit = hit | (picks[k:k + 1, :] == row)
            pick = jnp.where(hit, 1.0, 0.0).astype(jnp.bfloat16)
            d_buf[slot, r] = jnp.dot(pick, tokens, preferred_element_type=jnp.float32).astype(jnp.bfloat16)
            d_copy(m, s, slot, r).start()
        d_copy(m, s, slot, 0).wait()

    def dispatch_own(l, m, count):
        dispatch(l, m, iz, count)

    def dispatch_rest(l, m, count):
        def body(k, carry):
            s = row_of(k)
            gather_wait(m, s)
            dispatch(l, m, s, count + k)
            return carry
        lax.fori_loop(0, N_Z - 1, body, 0)

    def ffn(l, m, k, count):
        s = row_of(k)
        slot = count % SEND_SLOTS
        for r in range(1, N_PEER):
            d_copy(m, s, 0, r).wait_recv()
        load = pltpu.make_async_copy(d_land.at[m, s], stage, copy_sem)
        load.start()
        buffer_free(r_copy, m, s, count)
        load.wait()

        def one_expert(j, carry):
            at = pl.multiple_of(j * capacity, 16)
            rows = stage[:, pl.ds(at, capacity), :].reshape(N_PEER * capacity, hidden)
            gate_in = jnp.dot(rows, v_up1[j], preferred_element_type=jnp.float32)
            lin_in = jnp.dot(rows, v_up3[j], preferred_element_type=jnp.float32)
            act = (jax.nn.silu(gate_in) * lin_in).astype(jnp.bfloat16)
            res = jnp.dot(act, v_down[j], preferred_element_type=jnp.float32).astype(jnp.bfloat16)
            r_buf[slot, :, pl.ds(at, capacity), :] = res.reshape(N_PEER, capacity, hidden)
            return carry
        lax.fori_loop(0, 2 * exp_dev, one_expert, 0)
        for r in range(1, N_PEER):
            r_copy(m, s, slot, r).start()
        r_copy(m, s, slot, 0).start()
        r_copy(m, s, slot, 0).wait()

    def chain_copy(m, s, kind, to_inner):
        return remote(part.at[s], c_land.at[m, kind], c_send.at[s], c_recv.at[m, kind], along_z(inner_z if to_inner else outer_z))

    def chain_arrival(m, kind):
        remote(sum_stage, c_land.at[m, kind], c_send.at[0], c_recv.at[m, kind], partner).wait_recv()
        load = pltpu.make_async_copy(c_land.at[m, kind], sum_stage, copy_sem)
        load.start()
        load.wait()

    def part_sent(m, s):
        chain_copy(m, s, 0, True).wait_send()

    def combine(l, m, k, first):
        s = row_of(k)
        for r in range(1, N_PEER):
            r_copy(m, s, 0, r).wait_recv()
        load = pltpu.make_async_copy(r_land.at[m, s], stage, copy_sem)
        load.start()
        lane = lax.broadcasted_iota(jnp.int32, (1, N_PEER * block), 1)
        target = lane
        for r in range(N_PEER):
            py, px = peer_chip(r)
            inside = (lane >= r * block) & (lane < (r + 1) * block)
            target = jnp.where(inside, lane + (py * 2 + px - r) * block, target)
        picks, gates = slots_col[l, m, s], gates_col[l, m, s]
        weight = jnp.zeros((tok_mb, N_PEER * block), jnp.float32)
        for j in range(top_k):
            weight = weight + jnp.where(picks[:, j:j + 1] == target, gates[:, j:j + 1], 0.0)
        high = weight.astype(jnp.bfloat16)
        w_hi[...] = high
        w_lo[...] = (weight - high.astype(jnp.float32)).astype(jnp.bfloat16)
        if not first:
            @pl.when(k < N_Z - 1)
            def _():
                part_sent(m, s)
        load.wait()

        def one_column(n, carry):
            cols = pl.ds(pl.multiple_of(n * column, column), column)
            rows = stage[:, :, cols].reshape(N_PEER * block, column)
            total = jnp.dot(w_hi[...], rows, preferred_element_type=jnp.float32)
            total = total + jnp.dot(w_lo[...], rows, preferred_element_type=jnp.float32)
            part[s, :, cols] = total
            return carry
        lax.fori_loop(0, hidden // column, one_column, 0)

        @pl.when(is_end & (k < N_Z - 1))
        def _():
            chain_copy(m, s, k, True).start()

    def forward(m, step):
        @pl.when(is_mid)
        def _():
            s = row_of(step)
            chain_arrival(m, (0, 1, 3)[step])
            part[s] = part[s] + sum_stage[...]
            chain_copy(m, s, (3, 4, 4)[step], step < 2).start()

    def combine_step(l, m, k, first):
        combine(l, m, k, first)
        for step in range(N_Z - 1):
            @pl.when(k == step + 1)
            def _():
                forward(m, step)

    def finish(m):
        gather_sent(m)

        @pl.when(is_mid)
        def _():
            chain_arrival(m, 2)
            part[iz] = part[iz] + sum_stage[...]
        chain_arrival(m, 4)
        total = part[iz] + sum_stage[...]
        col[m, iz] = (col[m, iz].astype(jnp.float32) + ROUTE_SCALE * total).astype(jnp.bfloat16)

    sources = (w_up1, w_up3, w_down)
    crossed = (x_up1, x_up3, x_down)
    resident = (v_up1, v_up3, v_down)

    def cross_copy(l, a):
        return remote(sources[a].at[l], crossed[a].at[l], x_send.at[l, a], x_recv.at[l, a], partner)

    def weight_loads(l):
        own = [pltpu.make_async_copy(sources[a].at[l], resident[a].at[pl.ds(ic * exp_dev, exp_dev)], load_sem.at[a, 0]) for a in range(3)]
        other = [pltpu.make_async_copy(crossed[a].at[l], resident[a].at[pl.ds((1 - ic) * exp_dev, exp_dev)], load_sem.at[a, 1]) for a in range(3)]
        return own, other

    def weights_start(l):
        own, other = weight_loads(l)
        for copy in own:
            copy.start()
        for a in range(3):
            cross_copy(l, a).wait_recv()
            other[a].start()

    def weights_wait(l):
        own, other = weight_loads(l)
        for copy in own + other:
            copy.wait()

    first_load = [pltpu.make_async_copy(tok_in.at[m], col.at[m, iz], load_sem.at[m, 0]) for m in range(n_micro)]
    for copy in first_load:
        copy.start()
    for m in range(n_micro):
        first_load[m].wait()
        gather_start(m)
    for l in range(n_layers):
        for a in range(3):
            cross_copy(l, a).start()
    dispatch_own(0, 0, 0)
    dispatch_rest(0, 0, 1)
    weights_start(0)
    for l in range(n_layers):
        base = l * 2 * N_Z
        dispatch_own(l, 1, base + N_Z)
        weights_wait(l)

        def ffn_first(k, carry):
            ffn(l, 0, k, base + k)
            return carry
        lax.fori_loop(0, N_Z, ffn_first, 0)
        dispatch_rest(l, 1, base + N_Z + 1)

        def ffn_second(k, carry):
            ffn(l, 1, k, base + N_Z + k)
            combine_step(l, 0, k, l == 0)
            return carry
        lax.fori_loop(0, N_Z, ffn_second, 0)
        last = l == n_layers - 1
        if not last:
            weights_start(l + 1)
        finish(0)
        if not last:
            gather_start(0)
            dispatch_own(l + 1, 0, base + 2 * N_Z)

        def combine_second(k, carry):
            combine_step(l, 1, k, False)
            return carry
        lax.fori_loop(0, N_Z, combine_second, 0)
        if not last:
            dispatch_rest(l + 1, 0, base + 2 * N_Z + 1)
        finish(1)
        if not last:
            gather_start(1)

    results = [pltpu.make_async_copy(col.at[m, iz], out.at[m], load_sem.at[m, 0]) for m in range(n_micro)]
    for copy in results:
        copy.start()
    for slot in range(SEND_SLOTS):
        for r in range(1, N_PEER):
            d_copy(0, 0, slot, r).wait_send()
            r_copy(0, 0, slot, r).wait_send()
    for k in range(N_Z - 1):
        part_sent(0, row_of(k))
    for l in range(n_layers):
        for a in range(3):
            cross_copy(l, a).wait_send()
    for copy in results:
        copy.wait()


def solution(mesh):
    n_dev = mesh.shape["ez"] * mesh.shape["ey"] * mesh.shape["ex"]
    tok_spec = P(None, MESH_AXES, None)
    route_spec = P(None, None, MESH_AXES, None)
    weight_spec = P(None, MESH_AXES, None, None)

    def device_body(tokens_in, expert_ids, gate_vals, w_up1, w_up3, w_down):
        n_layers, n_micro, tok_mb, top_k = expert_ids.shape
        exp_dev = w_up1.shape[1]
        hidden, ffn_dim = w_up1.shape[2:]
        experts = exp_dev * n_dev
        capacity = capacity_of(tok_mb, top_k, experts)
        block = 2 * exp_dev * capacity
        slots = slot_table(expert_ids, experts, capacity)
        routes = jnp.concatenate([slots.astype(jnp.float32), gate_vals], axis=-1)
        routes = lax.all_gather(routes, "ez", axis=2)
        slots = routes[..., :top_k].astype(jnp.int32) - lax.axis_index("ez") * (N_PEER * block)
        gates = routes[..., top_k:]
        vmem, any_space = pl.BlockSpec(memory_space=pltpu.VMEM), pl.BlockSpec(memory_space=pl.ANY)
        bf16, f32, dma = jnp.bfloat16, jnp.float32, pltpu.SemaphoreType.DMA
        rows_shape = jax.ShapeDtypeStruct((n_micro, N_Z, N_PEER, block, hidden), bf16)
        outs = pl.pallas_call(
            functools.partial(moe_kernel, capacity),
            in_specs=[any_space, vmem, vmem, vmem, any_space, any_space, any_space],
            out_specs=[any_space] * 7,
            out_shape=[
                jax.ShapeDtypeStruct(tokens_in.shape, bf16),
                rows_shape,
                rows_shape,
                jax.ShapeDtypeStruct((n_micro, 5, tok_mb, hidden), f32),
                jax.ShapeDtypeStruct(w_up1.shape, bf16),
                jax.ShapeDtypeStruct(w_up3.shape, bf16),
                jax.ShapeDtypeStruct(w_down.shape, bf16),
            ],
            scratch_shapes=[
                pltpu.VMEM((n_micro, N_Z, tok_mb, hidden), bf16),
                pltpu.VMEM((SEND_SLOTS, N_PEER, block, hidden), bf16),
                pltpu.VMEM((SEND_SLOTS, N_PEER, block, hidden), bf16),
                pltpu.VMEM((N_Z, tok_mb, hidden), f32),
                pltpu.VMEM((2 * exp_dev, hidden, ffn_dim), bf16),
                pltpu.VMEM((2 * exp_dev, hidden, ffn_dim), bf16),
                pltpu.VMEM((2 * exp_dev, ffn_dim, hidden), bf16),
                pltpu.VMEM((N_PEER, block, hidden), bf16),
                pltpu.VMEM((tok_mb, hidden), f32),
                pltpu.VMEM((tok_mb, N_PEER * block), bf16),
                pltpu.VMEM((tok_mb, N_PEER * block), bf16),
                dma((n_micro, N_Z - 1)),
                dma((n_micro, N_Z)),
                dma((SEND_SLOTS, N_PEER)),
                dma((n_micro, N_Z, N_PEER)),
                dma((SEND_SLOTS, N_PEER)),
                dma((n_micro, N_Z, N_PEER)),
                dma((N_Z,)),
                dma((n_micro, 5)),
                dma((n_layers, 3)),
                dma((n_layers, 3)),
                dma((3, 2)),
                dma(()),
                dma(()),
            ],
            compiler_params=pltpu.CompilerParams(collective_id=0, has_side_effects=True, vmem_limit_bytes=VMEM_LIMIT),
            name="moe_layers",
        )(tokens_in, jnp.swapaxes(slots, -1, -2), slots, gates, w_up1, w_up3, w_down)
        return outs[0]

    return jax.shard_map(device_body, mesh=mesh, in_specs=(tok_spec, route_spec, route_spec, weight_spec, weight_spec, weight_spec), out_specs=tok_spec, check_vma=False)
```

time: 1720 us -> 1040 us (0.60)
  waiting for transfers between devices: 1370 us -> 0 us
  Pallas kernels: 0 us -> 999 us
  matrix products: 165 us -> 0 us
  starting transfers between devices: 96.9 us -> 0 us
  other arithmetic: 38.1 us -> 6.25 us
  local copies, waits for them, and re-layouts: 34.5 us -> 10.1 us
    all_to_all x8 -> x0, waiting for transfers between devices: 1370 us -> none  [the longest x4 686 us: device_body(): recv_buf = lax.all_to_all(send_buf, MESH_AXES, 0, 0, tiled=True)]
    pallas_call x0 -> x1, Pallas kernels: none -> 999 us  [device_body(): pl.pallas_call(functools.partial(moe_kernel, capacity), in_specs=[any_spa...]
    dot_general x16 -> x0, matrix products: 165 us -> none  [the longest x4 72.4 us: expert_ffn(): jnp.einsum('dkcf,kfh->dkch', hidden, mat_down, preferred_element_type=jnp...]
    all_to_all x8 -> x0, starting transfers between devices: 96.9 us -> none  [the longest x4 51.2 us: device_body(): returned = lax.all_to_all(expert_out, MESH_AXES, 0, 0, tiled=True)]
    convert_element_type x4 -> x0, local copies, waits for them, and re-layouts: 32.8 us -> none  [expert_ffn(): jnp.einsum('dkcf,kfh->dkch', hidden, mat_down, preferred_element_type=jnp...]
  transfers between devices with their start and end apart: 8 -> 0, of which waited for: 8 -> 0; matrix products, arithmetic and copies ran while one was open for 13% -> 0% of each run, Pallas kernels for 0% -> 0%
where the time goes in v2:
time: 1040 us; the launch traced here: 1030 us
  Pallas kernels  999 us (96%)
  blocking collectives  15.5 us (1%)
    pallas_call x1, Pallas kernels, device_body(): pl.pallas_call(functools.partial(moe_kernel, capacity), in_specs=[any_spa...  999 us

profile of v2, /device:TPU:0, one launch (start us, length us, event | category | flops | bytes accessed | tf_op | source)
XLA Modules:
  0.0 1031.0 jit_solution(3713527113109257707)
XLA Ops:
  0.0 0.0 copy-start
  0.0 0.8 copy.16
  0.8 0.7 copy.20
  1.6 0.2 convert_reduce_fusion
  1.8 2.4 reduce-window.6
  4.2 0.3 slice_reduce_fusion
  4.6 0.1 fusion.1
  4.7 0.2 select_reduce_fusion
  5.0 0.0 copy-done
  5.0 15.5 %all-gather = f32[2,2,1024,12]{2,3,1,0:T(8,128)S(1)} all-gather(f32[2,2,256,12]{2,3,1,0:T(8,128)S(1)} %pad_maximum_fusion), channel_id=2, replica_groups=mesh['ez'=4,'ey'=2,'ex'=4] {'ez'}, dimensions={2}, use_global_device_ids=true | all-gather | bytes 245760 | tf_op jit(solution)/shard_map/all_gather | solution.py:338
  20.5 0.6 copy.21
  21.2 1.6 fusion.2
  22.8 2.9 copy.22.slots_row
  25.7 1.6 fusion.slots_col
  27.3 2.0 slice.19.gates_col
  29.2 999.1 %moe_layers.1 = (bf16[2,256,1536]{2,1,0:T(8,128)(2,1)}, bf16[2,4,4,192,1536]{4,3,2,1,0:T(8,128)(2,1)}, bf16[2,4,4,192,1536]{4,3,2,1,0:T(8,128)(2,1)}, f32[2,5,25...) custom-call(bf16[2,256,1536]{2,1,0:T(8,128)(2,1)} %tok_in.1, ...), custom_call_target="tpu_custom_call" | custom-call | tf_op jit(solution)/shard_map/moe_layers/pallas_call | solution.py:344
  1028.4 2.7 copy.29
  (5 shorter events, 0.1 us)
Async XLA Ops:
  0.0 5.0 copy-start

commit v3 on v2

v3 whole, which is shorter than its diff:
```python
import functools

import jax
import jax.numpy as jnp
from jax import lax
from jax.experimental import pallas as pl
from jax.experimental.pallas import tpu as pltpu
from jax.sharding import PartitionSpec as P

ROUTE_SCALE = 2.5
MESH_AXES = ("ez", "ey", "ex")
N_Z = 4
N_PEER = 4
D_SLOTS = 6
R_SLOTS = 3
VMEM_LIMIT = 67043328
COLUMN = 512


def capacity_of(tok_mb, top_k, experts):
    return 2 * ((tok_mb * top_k + experts - 1) // experts)


def slot_table(ids, experts, capacity):
    chosen = (ids[..., None] == jnp.arange(experts)).astype(jnp.int32)
    per_expert = jnp.sum(chosen, axis=-2)
    token_rank = jnp.cumsum(per_expert, axis=-2) - per_expert
    slot_pos = jnp.sum(chosen * token_rank[..., None, :], axis=-1)
    return ids * capacity + slot_pos


def moe_kernel(capacity, top_k, tok_in, routes_in, w_up1, w_up3, w_down,
               out, d_land, r_land, c_land, x_up1, x_up3, x_down,
               col, d_buf, r_buf, part, v_up1, v_up3, v_down, stage, sum_stage, w_hi, w_lo, routes, routes_near,
               swap_send, ag_send, ag_recv, d_send, d_recv, r_send, r_recv, c_send, c_recv, x_send, x_recv,
               t_send, t_recv, n_send, n_recv, load_sem, copy_sem, self_sem):
    n_micro, n_layers = routes_in.shape[:2]
    tok_mb = routes_in.shape[3]
    hidden = col.shape[-1]
    exp_dev = w_up1.shape[1]
    block = d_buf.shape[2]
    column = min(COLUMN, hidden)
    iz, iy, ie = lax.axis_index("ez"), lax.axis_index("ey"), lax.axis_index("ex")
    ix, ic = ie // 2, ie % 2
    edge = jnp.minimum(iz, N_Z - 1 - iz)
    low = iz < N_Z // 2
    is_end = edge == 0
    is_mid = edge == 1
    mesh_id = pl.DeviceIdType.MESH

    def peer_chip(r):
        return (iy + r // 2) % 2, (ix + r % 2) % 2

    def peer(r, z=None):
        py, px = peer_chip(r)
        return (iz if z is None else z, py, px * 2 + ic)

    def near_axis(s):
        return 1 + s % 2

    def far_axis(s):
        return 2 - s % 2

    def relation(s, i):
        return (0, near_axis(s), far_axis(s), 3)[i]

    partner = (iz, iy, ix * 2 + (1 - ic))
    inner_z = jnp.where(low, jnp.where(is_end, 1, 2), jnp.where(is_end, 2, 1))
    outer_z = jnp.where(low, 0, N_Z - 1)

    def row_of(k):
        pos = jnp.where(k == 0, 3, jnp.where(k == 1, 2, jnp.where(k == 2, 1 - edge, edge)))
        return jnp.where(low, pos, N_Z - 1 - pos)

    def near_row(j):
        pos = jnp.where(j == 0, 1 - edge, j + 1)
        return jnp.where(low, pos, N_Z - 1 - pos)

    barrier = pltpu.get_barrier_semaphore()
    for r in range(1, N_PEER):
        pl.semaphore_signal(barrier, inc=1, device_id=peer(r), device_id_type=mesh_id)
    for t in range(1, N_Z):
        z = (iz + t) % N_Z
        pl.semaphore_signal(barrier, inc=1, device_id=peer(0, z), device_id_type=mesh_id)
        pl.semaphore_signal(barrier, inc=1, device_id=peer(near_axis(z), z), device_id_type=mesh_id)
    pl.semaphore_signal(barrier, inc=1, device_id=partner, device_id_type=mesh_id)
    pl.semaphore_wait(barrier, N_PEER + 2 * (N_Z - 1))

    def remote(src, dst, send_sem, recv_sem, device):
        return pltpu.make_async_remote_copy(src_ref=src, dst_ref=dst, send_sem=send_sem, recv_sem=recv_sem, device_id=device, device_id_type=mesh_id)

    def table_copy(t):
        return remote(routes_in, routes.at[iz], t_send.at[t - 1], t_recv.at[iz], peer(0, (iz + t) % N_Z))

    def near_table_copy(t):
        return remote(routes_in, routes_near.at[iz], n_send.at[t], n_recv.at[iz], peer(near_axis(iz), (iz + t) % N_Z))

    def tables_wait():
        for t in range(1, N_Z):
            z = (iz + t) % N_Z
            remote(routes_in, routes.at[z], t_send.at[0], t_recv.at[z], partner).wait_recv()
        for z in range(N_Z):
            remote(routes_in, routes_near.at[z], n_send.at[0], n_recv.at[z], partner).wait_recv()

    def swap_copy(m):
        return remote(col.at[m, 0, iz], col.at[m, 1, iz], swap_send.at[m], ag_recv.at[m, 1, iz], peer(near_axis(iz)))

    def gather_copy(m, t, s, to_inner, sem):
        return remote(col.at[m, t, s], col.at[m, t, s], ag_send.at[m, t, sem], ag_recv.at[m, t, s], peer(0, inner_z if to_inner else outer_z))

    def gather_wait(m, t, s):
        remote(col.at[m, t, s], col.at[m, t, s], ag_send.at[m, t, 0], ag_recv.at[m, t, s], partner).wait_recv()

    def gather_start(m, t):
        @pl.when(is_mid)
        def _():
            gather_copy(m, t, iz, False, 1).start()
        gather_copy(m, t, iz, True, 0).start()

    def pump(m, j):
        s = near_row(j)
        for t in range(2):
            gather_wait(m, t, s)

            @pl.when(is_mid)
            def _():
                gather_copy(m, t, s, j == 0, 2 + j).start()

    def gather_sent(m):
        swap_copy(m).wait_send()
        for t in range(2):
            gather_copy(m, t, iz, True, 0).wait_send()

            @pl.when(is_mid)
            def _():
                for sem in range(1, 2 + N_Z - 1):
                    gather_copy(m, t, iz, False, sem).wait_send()

    def d_self(m, t, s, slot):
        return pltpu.make_async_copy(d_buf.at[slot, 0], d_land.at[m, s, t], self_sem)

    def d_copy(m, t, s, slot):
        return remote(d_buf.at[slot, 1], d_land.at[m, s, 2 + t], d_send.at[slot], d_recv.at[m, s, t], peer(far_axis(s)))

    def r_copy(m, s, slot, i):
        if i == 0:
            return pltpu.make_async_copy(r_buf.at[slot, 0], r_land.at[m, s, 0], self_sem)
        return remote(r_buf.at[slot, i], r_land.at[m, s, i], r_send.at[slot, i], r_recv.at[m, s, i], peer(relation(s, i)))

    def dispatch(l, m, t, s, count):
        slot = count % D_SLOTS

        @pl.when(count >= D_SLOTS)
        def _():
            d_copy(m, t, s, slot).wait_send()
        tokens = col[m, t, s]
        picks = (routes_near if t else routes)[s, m, l]
        row = lax.broadcasted_iota(jnp.int32, (block, tok_mb), 0)
        for dest in (1, 0):
            py, px = peer_chip(far_axis(s) if dest else 0)
            first = iz * (N_PEER * block) + (py * 2 + px) * block
            wanted = (row + first).astype(jnp.float32)
            hit = jnp.zeros((block, tok_mb), jnp.bool_)
            for k in range(top_k):
                hit = hit | (picks[k:k + 1, :] == wanted)
            pick = jnp.where(hit, 1.0, 0.0).astype(jnp.bfloat16)
            d_buf[slot, dest] = jnp.dot(pick, tokens, preferred_element_type=jnp.float32).astype(jnp.bfloat16)
            if dest:
                d_copy(m, t, s, slot).start()
        d_self(m, t, s, slot).start()
        d_self(m, t, s, slot).wait()

    def dispatch_near(l, m, count):
        gather_wait(m, 1, iz)
        gather_start(m, 1)
        dispatch(l, m, 1, iz, count)

    def dispatch_row(l, m, j, count):
        for t in range(2):
            dispatch(l, m, t, near_row(j), count + t)

    def dispatch_rest(l, m, count):
        def body(j, carry):
            dispatch_row(l, m, j, count + 2 * j)
            return carry
        lax.fori_loop(0, N_Z - 1, body, 0)

    def ffn(l, m, k, count):
        s = row_of(k)
        slot = count % R_SLOTS
        for t in range(2):
            d_copy(m, t, s, 0).wait_recv()
        load = pltpu.make_async_copy(d_land.at[m, s], stage, copy_sem)
        load.start()

        @pl.when(count >= R_SLOTS)
        def _():
            for i in range(1, N_PEER):
                r_copy(m, s, slot, i).wait_send()
        load.wait()

        def one_expert(j, carry):
            at = pl.multiple_of(j * capacity, 16)
            rows = stage[:, pl.ds(at, capacity), :].reshape(N_PEER * capacity, hidden)
            gate_in = jnp.dot(rows, v_up1[j], preferred_element_type=jnp.float32)
            lin_in = jnp.dot(rows, v_up3[j], preferred_element_type=jnp.float32)
            act = (jax.nn.silu(gate_in) * lin_in).astype(jnp.bfloat16)
            res = jnp.dot(act, v_down[j], preferred_element_type=jnp.float32).astype(jnp.bfloat16)
            r_buf[slot, :, pl.ds(at, capacity), :] = res.reshape(N_PEER, capacity, hidden)
            return carry
        lax.fori_loop(0, 2 * exp_dev, one_expert, 0)
        for i in (3, 1, 2, 0):
            r_copy(m, s, slot, i).start()
        r_copy(m, s, slot, 0).wait()

    def chain_copy(m, s, kind, to_inner):
        return remote(part.at[s], c_land.at[m, kind], c_send.at[s], c_recv.at[m, kind], peer(0, inner_z if to_inner else outer_z))

    def chain_arrival(m, kind):
        remote(sum_stage, c_land.at[m, kind], c_send.at[0], c_recv.at[m, kind], partner).wait_recv()
        load = pltpu.make_async_copy(c_land.at[m, kind], sum_stage, copy_sem)
        load.start()
        load.wait()

    def part_sent(m, s):
        chain_copy(m, s, 0, True).wait_send()

    def combine(l, m, k, first):
        s = row_of(k)
        for i in range(1, N_PEER):
            r_copy(m, s, 0, i).wait_recv()
        load = pltpu.make_async_copy(r_land.at[m, s], stage, copy_sem)
        load.start()
        line = lax.broadcasted_iota(jnp.int32, (N_PEER * block, tok_mb), 0)
        target = line
        for i in range(N_PEER):
            py, px = peer_chip(relation(s, i))
            inside = (line >= i * block) & (line < (i + 1) * block)
            target = jnp.where(inside, line + (iz * (N_PEER * block) + (py * 2 + px - i) * block), target)
        target = target.astype(jnp.float32)
        table = routes[s, m, l]
        weight = jnp.zeros((N_PEER * block, tok_mb), jnp.float32)
        for j in range(top_k):
            weight = weight + jnp.where(table[j:j + 1, :] == target, table[8 + j:9 + j, :], 0.0)
        weight = weight.T
        high = weight.astype(jnp.bfloat16)
        w_hi[...] = high
        w_lo[...] = (weight - high.astype(jnp.float32)).astype(jnp.bfloat16)
        if not first:
            @pl.when(k < N_Z - 1)
            def _():
                part_sent(m, s)
        load.wait()

        def one_column(n, carry):
            cols = pl.ds(pl.multiple_of(n * column, column), column)
            rows = stage[:, :, cols].reshape(N_PEER * block, column)
            total = jnp.dot(w_hi[...], rows, preferred_element_type=jnp.float32)
            total = total + jnp.dot(w_lo[...], rows, preferred_element_type=jnp.float32)
            part[s, :, cols] = total
            return carry
        lax.fori_loop(0, hidden // column, one_column, 0)

        @pl.when(is_end & (k < N_Z - 1))
        def _():
            chain_copy(m, s, k, True).start()

    def forward(m, step):
        @pl.when(is_mid)
        def _():
            s = row_of(step)
            chain_arrival(m, (0, 1, 3)[step])
            part[s] = part[s] + sum_stage[...]
            chain_copy(m, s, (3, 4, 4)[step], step < 2).start()

    def combine_step(l, m, k, first):
        combine(l, m, k, first)
        for step in range(N_Z - 1):
            @pl.when(k == step + 1)
            def _():
                forward(m, step)

    def intake_step(l, m, k, count):
        @pl.when(k == 0)
        def _():
            dispatch_near(l, m, count)
        for j in range(N_Z - 1):
            @pl.when(k == j + 1)
            def _():
                pump(m, j)

    def finish(m):
        @pl.when(is_mid)
        def _():
            chain_arrival(m, 2)
            part[iz] = part[iz] + sum_stage[...]
        chain_arrival(m, 4)
        total = part[iz] + sum_stage[...]
        col[m, 0, iz] = (col[m, 0, iz].astype(jnp.float32) + ROUTE_SCALE * total).astype(jnp.bfloat16)

    def share(m):
        swap_copy(m).start()
        gather_start(m, 0)

    sources = (w_up1, w_up3, w_down)
    crossed = (x_up1, x_up3, x_down)
    resident = (v_up1, v_up3, v_down)

    def cross_copy(l, a):
        return remote(sources[a].at[l], crossed[a].at[l], x_send.at[l, a], x_recv.at[l, a], partner)

    def weight_loads(l):
        own = [pltpu.make_async_copy(sources[a].at[l], resident[a].at[pl.ds(ic * exp_dev, exp_dev)], load_sem.at[a, 0]) for a in range(3)]
        other = [pltpu.make_async_copy(crossed[a].at[l], resident[a].at[pl.ds((1 - ic) * exp_dev, exp_dev)], load_sem.at[a, 1]) for a in range(3)]
        return own, other

    def weights_start(l):
        own, other = weight_loads(l)
        for copy in own:
            copy.start()
        for a in range(3):
            cross_copy(l, a).wait_recv()
            other[a].start()

    def weights_wait(l):
        own, other = weight_loads(l)
        for copy in own + other:
            copy.wait()

    first_load = [pltpu.make_async_copy(tok_in.at[m], col.at[m, 0, iz], load_sem.at[m, 0]) for m in range(n_micro)]
    for copy in first_load:
        copy.start()
    for t in range(1, N_Z):
        table_copy(t).start()
    for t in range(N_Z):
        near_table_copy(t).start()
    for m in range(n_micro):
        first_load[m].wait()
        swap_copy(m).start()
        if m == 0:
            gather_start(0, 0)
    for l in range(n_layers):
        for a in range(3):
            cross_copy(l, a).start()
    routes[iz] = routes_in[...]
    tables_wait()
    dispatch(0, 0, 0, iz, 0)
    dispatch_near(0, 0, 1)
    gather_start(1, 0)
    for j in range(N_Z - 1):
        pump(0, j)
        dispatch_row(0, 0, j, 2 + 2 * j)
    weights_start(0)
    for l in range(n_layers):
        last = l == n_layers - 1
        d_base, r_base = l * 4 * N_Z, l * 2 * N_Z
        d_other, d_next = d_base + 2 * N_Z, d_base + 4 * N_Z
        dispatch(l, 1, 0, iz, d_other)
        weights_wait(l)
        gather_sent(0)

        def ffn_first(k, carry):
            ffn(l, 0, k, r_base + k)
            intake_step(l, 1, k, d_other + 1)
            return carry
        lax.fori_loop(0, N_Z, ffn_first, 0)
        dispatch_rest(l, 1, d_other + 2)
        gather_sent(1)

        def ffn_second(k, carry):
            ffn(l, 1, k, r_base + N_Z + k)
            combine_step(l, 0, k, l == 0)
            return carry
        lax.fori_loop(0, N_Z, ffn_second, 0)
        if not last:
            weights_start(l + 1)
        finish(0)
        if not last:
            share(0)
            dispatch(l + 1, 0, 0, iz, d_next)

        def combine_second(k, carry):
            combine_step(l, 1, k, False)
            if not last:
                intake_step(l + 1, 0, k, d_next + 1)
            return carry
        lax.fori_loop(0, N_Z, combine_second, 0)
        if not last:
            dispatch_rest(l + 1, 0, d_next + 2)
        finish(1)
        if not last:
            share(1)

    results = [pltpu.make_async_copy(col.at[m, 0, iz], out.at[m], load_sem.at[m, 0]) for m in range(n_micro)]
    for copy in results:
        copy.start()
    for slot in range(D_SLOTS):
        d_copy(0, 0, iz, slot).wait_send()
    for slot in range(R_SLOTS):
        for i in range(1, N_PEER):
            r_copy(0, iz, slot, i).wait_send()
    for k in range(N_Z - 1):
        part_sent(0, row_of(k))
    for l in range(n_layers):
        for a in range(3):
            cross_copy(l, a).wait_send()
    for t in range(1, N_Z):
        table_copy(t).wait_send()
    for t in range(N_Z):
        near_table_copy(t).wait_send()
    for copy in results:
        copy.wait()


def solution(mesh):
    n_dev = mesh.shape["ez"] * mesh.shape["ey"] * mesh.shape["ex"]
    tok_spec = P(None, MESH_AXES, None)
    route_spec = P(None, None, MESH_AXES, None)
    weight_spec = P(None, MESH_AXES, None, None)

    def device_body(tokens_in, expert_ids, gate_vals, w_up1, w_up3, w_down):
        n_layers, n_micro, tok_mb, top_k = expert_ids.shape
        exp_dev = w_up1.shape[1]
        hidden, ffn_dim = w_up1.shape[2:]
        experts = exp_dev * n_dev
        capacity = capacity_of(tok_mb, top_k, experts)
        block = 2 * exp_dev * capacity
        slots = slot_table(expert_ids, experts, capacity)
        pad = ((0, 0), (0, 0), (0, 0), (0, 8 - top_k))
        routes = jnp.concatenate([jnp.pad(slots.astype(jnp.float32), pad), jnp.pad(gate_vals, pad)], axis=-1)
        routes = jnp.transpose(routes, (1, 0, 3, 2))
        vmem, any_space = pl.BlockSpec(memory_space=pltpu.VMEM), pl.BlockSpec(memory_space=pl.ANY)
        bf16, f32, dma = jnp.bfloat16, jnp.float32, pltpu.SemaphoreType.DMA
        rows_shape = jax.ShapeDtypeStruct((n_micro, N_Z, N_PEER, block, hidden), bf16)
        outs = pl.pallas_call(
            functools.partial(moe_kernel, capacity, top_k),
            in_specs=[any_space, vmem, any_space, any_space, any_space],
            out_specs=[any_space] * 7,
            out_shape=[
                jax.ShapeDtypeStruct(tokens_in.shape, bf16),
                rows_shape,
                rows_shape,
                jax.ShapeDtypeStruct((n_micro, 5, tok_mb, hidden), f32),
                jax.ShapeDtypeStruct(w_up1.shape, bf16),
                jax.ShapeDtypeStruct(w_up3.shape, bf16),
                jax.ShapeDtypeStruct(w_down.shape, bf16),
            ],
            scratch_shapes=[
                pltpu.VMEM((n_micro, 2, N_Z, tok_mb, hidden), bf16),
                pltpu.VMEM((D_SLOTS, 2, block, hidden), bf16),
                pltpu.VMEM((R_SLOTS, N_PEER, block, hidden), bf16),
                pltpu.VMEM((N_Z, tok_mb, hidden), f32),
                pltpu.VMEM((2 * exp_dev, hidden, ffn_dim), bf16),
                pltpu.VMEM((2 * exp_dev, hidden, ffn_dim), bf16),
                pltpu.VMEM((2 * exp_dev, ffn_dim, hidden), bf16),
                pltpu.VMEM((N_PEER, block, hidden), bf16),
                pltpu.VMEM((tok_mb, hidden), f32),
                pltpu.VMEM((tok_mb, N_PEER * block), bf16),
                pltpu.VMEM((tok_mb, N_PEER * block), bf16),
                pltpu.VMEM((N_Z,) + routes.shape, f32),
                pltpu.VMEM((N_Z,) + routes.shape, f32),
                dma((n_micro,)),
                dma((n_micro, 2, N_Z + 1)),
                dma((n_micro, 2, N_Z)),
                dma((D_SLOTS,)),
                dma((n_micro, N_Z, 2)),
                dma((R_SLOTS, N_PEER)),
                dma((n_micro, N_Z, N_PEER)),
                dma((N_Z,)),
                dma((n_micro, 5)),
                dma((n_layers, 3)),
                dma((n_layers, 3)),
                dma((N_Z - 1,)),
                dma((N_Z,)),
                dma((N_Z,)),
                dma((N_Z,)),
                dma((3, 2)),
                dma(()),
                dma(()),
            ],
            compiler_params=pltpu.CompilerParams(collective_id=0, has_side_effects=True, vmem_limit_bytes=VMEM_LIMIT),
            name="moe_layers",
        )(tokens_in, routes, w_up1, w_up3, w_down)
        return outs[0]

    return jax.shard_map(device_body, mesh=mesh, in_specs=(tok_spec, route_spec, route_spec, weight_spec, weight_spec, weight_spec), out_specs=tok_spec, check_vma=False)
```

time: 1040 us -> 1090 us (1.048)
  Pallas kernels: 999 us -> 1080 us
  blocking collectives: 15.5 us -> 0 us
    pallas_call x1, Pallas kernels: 999 us -> 1080 us  [device_body(): pl.pallas_call(functools.partial(moe_kernel, capacity, top_k), in_specs=[...]
    all_gather x1 -> x0, blocking collectives: 15.5 us -> none  [device_body(): routes = lax.all_gather(routes, 'ez', axis=2)]
where the time goes in v3:
time: 1090 us
  Pallas kernels  1080 us (99%)
    pallas_call x1, Pallas kernels, device_body(): pl.pallas_call(functools.partial(moe_kernel, capacity, top_k), in_specs=[...  1080 us

profile of v3, /device:TPU:0, one launch (start us, length us, event | category | flops | bytes accessed | tf_op | source)
XLA Modules:
  0.0 1088.8 jit_solution(878881818044931523)
XLA Ops:
  0.0 0.0 copy-start
  0.0 0.8 copy.17
  0.8 0.7 copy.21
  1.6 0.2 convert_reduce_fusion
  1.8 2.4 reduce-window.6
  4.2 0.3 slice_reduce_fusion
  4.6 0.1 fusion
  4.7 0.2 select_reduce_fusion
  5.0 0.0 copy-done
  5.0 0.6 fusion.1.routes_in
  5.6 1080.6 %moe_layers.1 = (bf16[2,256,1536]{2,1,0:T(8,128)(2,1)}, bf16[2,4,4,192,1536]{4,3,2,1,0:T(8,128)(2,1)}, bf16[2,4,4,192,1536]{4,3,2,1,0:T(8,128)(2,1)}, f32[2,5,25...) custom-call(bf16[2,256,1536]{2,1,0:T(8,128)(2,1)} %tok_in.1, ...), custom_call_target="tpu_custom_call" | custom-call | tf_op jit(solution)/shard_map/moe_layers/pallas_call | solution.py:435
  1086.2 2.7 copy.33
  (4 shorter events, 0.1 us)
Async XLA Ops:
  0.0 5.0 copy-start

commit v4 on v2

--- a/solution.py
+++ b/solution.py
@@ -11,7 +11,7 @@
 MESH_AXES = ("ez", "ey", "ex")
 N_Z = 4
 N_PEER = 4
-SEND_SLOTS = 3
+SEND_SLOTS = 4
 VMEM_LIMIT = 67043328
 COLUMN = 512
 
@@ -28,12 +28,13 @@
     return ids * capacity + slot_pos
 
 
-def moe_kernel(capacity, tok_in, slots_row, slots_col, gates_col, w_up1, w_up3, w_down,
+def moe_kernel(capacity, top_k, tok_in, routes_in, w_up1, w_up3, w_down,
                out, d_land, r_land, c_land, x_up1, x_up3, x_down,
-               col, d_buf, r_buf, part, v_up1, v_up3, v_down, stage, sum_stage, w_hi, w_lo,
-               ag_send, ag_recv, d_send, d_recv, r_send, r_recv, c_send, c_recv, x_send, x_recv, load_sem, copy_sem, self_sem):
-    n_layers, n_micro = slots_row.shape[:2]
-    top_k, tok_mb = slots_row.shape[3:]
+               col, d_buf, r_buf, part, v_up1, v_up3, v_down, stage, sum_stage, w_hi, w_lo, routes,
+               ag_send, ag_recv, d_send, d_recv, r_send, r_recv, c_send, c_recv, x_send, x_recv,
+               t_send, t_recv, load_sem, copy_sem, self_sem):
+    n_micro, n_layers = routes_in.shape[:2]
+    tok_mb = routes_in.shape[3]
     hidden = col.shape[-1]
     exp_dev = w_up1.shape[1]
     block = d_buf.shape[2]
@@ -49,12 +50,9 @@
     def peer_chip(r):
         return (iy + r // 2) % 2, (ix + r % 2) % 2
 
-    def peer(r):
+    def peer(r, z=None):
         py, px = peer_chip(r)
-        return (iz, py, px * 2 + ic)
-
-    def along_z(z):
-        return (z, iy, ie)
+        return (iz if z is None else z, py, px * 2 + ic)
 
     partner = (iz, iy, ix * 2 + (1 - ic))
     inner_z = jnp.where(low, jnp.where(is_end, 1, 2), jnp.where(is_end, 2, 1))
@@ -62,21 +60,34 @@
 
     def row_of(k):
         pos = jnp.where(k == 0, 3, jnp.where(k == 1, 2, jnp.where(k == 2, 1 - edge, edge)))
+        return jnp.where(low, pos, N_Z - 1 - pos)
+
+    def near_row(j):
+        pos = jnp.where(j == 0, 1 - edge, j + 1)
         return jnp.where(low, pos, N_Z - 1 - pos)
 
     barrier = pltpu.get_barrier_semaphore()
     for r in range(1, N_PEER):
         pl.semaphore_signal(barrier, inc=1, device_id=peer(r), device_id_type=mesh_id)
     for t in range(1, N_Z):
-        pl.semaphore_signal(barrier, inc=1, device_id=along_z((iz + t) % N_Z), device_id_type=mesh_id)
+        z = (iz + t) % N_Z
+        pl.semaphore_signal(barrier, inc=1, device_id=peer(0, z), device_id_type=mesh_id)
     pl.semaphore_signal(barrier, inc=1, device_id=partner, device_id_type=mesh_id)
     pl.semaphore_wait(barrier, N_PEER + N_Z - 1)
 
     def remote(src, dst, send_sem, recv_sem, device):
         return pltpu.make_async_remote_copy(src_ref=src, dst_ref=dst, send_sem=send_sem, recv_sem=recv_sem, device_id=device, device_id_type=mesh_id)
 
+    def table_copy(t):
+        return remote(routes_in, routes.at[iz], t_send.at[t - 1], t_recv.at[iz], peer(0, (iz + t) % N_Z))
+
+    def tables_wait():
+        for t in range(1, N_Z):
+            z = (iz + t) % N_Z
+            remote(routes_in, routes.at[z], t_send.at[0], t_recv.at[z], partner).wait_recv()
+
     def gather_copy(m, t):
-        return remote(col.at[m, iz], col.at[m, iz], ag_send.at[m, t - 1], ag_recv.at[m, iz], along_z((iz + t) % N_Z))
+        return remote(col.at[m, iz], col.at[m, iz], ag_send.at[m, t - 1], ag_recv.at[m, iz], peer(0, (iz + t) % N_Z))
 
     def gather_start(m):
         for t in (2, 1, 3):
@@ -109,28 +120,23 @@
         slot = count % SEND_SLOTS
         buffer_free(d_copy, m, s, count)
         tokens = col[m, s]
-        picks = slots_row[l, m, s]
-        for r in range(N_PEER):
+        picks = routes[s, m, l]
+        row = lax.broadcasted_iota(jnp.int32, (block, tok_mb), 0)
+        for r in (3, 1, 2, 0):
             py, px = peer_chip(r)
-            row = lax.broadcasted_iota(jnp.int32, (block, tok_mb), 0) + (py * 2 + px) * block
+            wanted = (row + (iz * (N_PEER * block) + (py * 2 + px) * block)).astype(jnp.float32)
             hit = jnp.zeros((block, tok_mb), jnp.bool_)
             for k in range(top_k):
-                hit = hit | (picks[k:k + 1, :] == row)
+                hit = hit | (picks[k:k + 1, :] == wanted)
             pick = jnp.where(hit, 1.0, 0.0).astype(jnp.bfloat16)
             d_buf[slot, r] = jnp.dot(pick, tokens, preferred_element_type=jnp.float32).astype(jnp.bfloat16)
             d_copy(m, s, slot, r).start()
         d_copy(m, s, slot, 0).wait()
 
-    def dispatch_own(l, m, count):
-        dispatch(l, m, iz, count)
-
-    def dispatch_rest(l, m, count):
-        def body(k, carry):
-            s = row_of(k)
-            gather_wait(m, s)
-            dispatch(l, m, s, count + k)
-            return carry
-        lax.fori_loop(0, N_Z - 1, body, 0)
+    def dispatch_row(l, m, j, count):
+        s = near_row(j)
+        gather_wait(m, s)
+        dispatch(l, m, s, count + 1 + j)
 
     def ffn(l, m, k, count):
         s = row_of(k)
@@ -152,13 +158,12 @@
             r_buf[slot, :, pl.ds(at, capacity), :] = res.reshape(N_PEER, capacity, hidden)
             return carry
         lax.fori_loop(0, 2 * exp_dev, one_expert, 0)
-        for r in range(1, N_PEER):
+        for r in (3, 1, 2, 0):
             r_copy(m, s, slot, r).start()
-        r_copy(m, s, slot, 0).start()
         r_copy(m, s, slot, 0).wait()
 
     def chain_copy(m, s, kind, to_inner):
-        return remote(part.at[s], c_land.at[m, kind], c_send.at[s], c_recv.at[m, kind], along_z(inner_z if to_inner else outer_z))
+        return remote(part.at[s], c_land.at[m, kind], c_send.at[s], c_recv.at[m, kind], peer(0, inner_z if to_inner else outer_z))
 
     def chain_arrival(m, kind):
         remote(sum_stage, c_land.at[m, kind], c_send.at[0], c_recv.at[m, kind], partner).wait_recv()
@@ -171,20 +176,22 @@
 
     def combine(l, m, k, first):
         s = row_of(k)
-        for r in range(1, N_PEER):
-            r_copy(m, s, 0, r).wait_recv()
+        for i in range(1, N_PEER):
+            r_copy(m, s, 0, i).wait_recv()
         load = pltpu.make_async_copy(r_land.at[m, s], stage, copy_sem)
         load.start()
-        lane = lax.broadcasted_iota(jnp.int32, (1, N_PEER * block), 1)
-        target = lane
-        for r in range(N_PEER):
-            py, px = peer_chip(r)
-            inside = (lane >= r * block) & (lane < (r + 1) * block)
-            target = jnp.where(inside, lane + (py * 2 + px - r) * block, target)
-        picks, gates = slots_col[l, m, s], gates_col[l, m, s]
-        weight = jnp.zeros((tok_mb, N_PEER * block), jnp.float32)
+        line = lax.broadcasted_iota(jnp.int32, (N_PEER * block, tok_mb), 0)
+        target = line
+        for i in range(N_PEER):
+            py, px = peer_chip(i)
+            inside = (line >= i * block) & (line < (i + 1) * block)
+            target = jnp.where(inside, line + (iz * (N_PEER * block) + (py * 2 + px - i) * block), target)
+        target = target.astype(jnp.float32)
+        table = routes[s, m, l]
+        weight = jnp.zeros((N_PEER * block, tok_mb), jnp.float32)
         for j in range(top_k):
-            weight = weight + jnp.where(picks[:, j:j + 1] == target, gates[:, j:j + 1], 0.0)
+            weight = weight + jnp.where(table[j:j + 1, :] == target, table[8 + j:9 + j, :], 0.0)
+        weight = weight.T
         high = weight.astype(jnp.bfloat16)
         w_hi[...] = high
         w_lo[...] = (weight - high.astype(jnp.float32)).astype(jnp.bfloat16)
@@ -261,61 +268,79 @@
     first_load = [pltpu.make_async_copy(tok_in.at[m], col.at[m, iz], load_sem.at[m, 0]) for m in range(n_micro)]
     for copy in first_load:
         copy.start()
-    for m in range(n_micro):
-        first_load[m].wait()
-        gather_start(m)
+    for t in range(1, N_Z):
+        table_copy(t).start()
+    first_load[0].wait()
+    gather_start(0)
     for l in range(n_layers):
         for a in range(3):
             cross_copy(l, a).start()
-    dispatch_own(0, 0, 0)
-    dispatch_rest(0, 0, 1)
+    routes[iz] = routes_in[...]
+    first_load[1].wait()
+    tables_wait()
+    dispatch(0, 0, iz, 0)
+    gather_start(1)
+
+    def first_rows(j, carry):
+        dispatch_row(0, 0, j, 0)
+        return carry
+    lax.fori_loop(0, N_Z - 1, first_rows, 0)
     weights_start(0)
-    for l in range(n_layers):
-        base = l * 2 * N_Z
-        dispatch_own(l, 1, base + N_Z)
-        weights_wait(l)
-
-        def ffn_first(k, carry):
-            ffn(l, 0, k, base + k)
+    weights_wait(0)
+
+    def first_ffn(k, carry):
+        ffn(0, 0, k, k)
+        return carry
+    lax.fori_loop(0, N_Z, first_ffn, 0)
+    turns = [(l, m) for l in range(n_layers) for m in range(n_micro)]
+    for turn in range(1, len(turns)):
+        (l, m), (l_prev, m_prev) = turns[turn], turns[turn - 1]
+        base = turn * N_Z
+        if m == 0:
+            weights_start(l)
+        dispatch(l, m, iz, base)
+
+        def sums_and_rows(k, carry):
+            combine_step(l_prev, m_prev, k, turn == 1)
+
+            @pl.when(k < N_Z - 1)
+            def _():
+                dispatch_row(l, m, k, base)
             return carry
-        lax.fori_loop(0, N_Z, ffn_first, 0)
-        dispatch_rest(l, 1, base + N_Z + 1)
-
-        def ffn_second(k, carry):
-            ffn(l, 1, k, base + N_Z + k)
-            combine_step(l, 0, k, l == 0)
+        lax.fori_loop(0, N_Z, sums_and_rows, 0)
+        if m == 0:
+            weights_wait(l)
+        ffn(l, m, 0, base)
+        finish(m_prev)
+        if l_prev < n_layers - 1:
+            gather_start(m_prev)
+
+        def rest_ffn(k, carry):
+            ffn(l, m, k, base + k)
             return carry
-        lax.fori_loop(0, N_Z, ffn_second, 0)
-        last = l == n_layers - 1
-        if not last:
-            weights_start(l + 1)
-        finish(0)
-        if not last:
-            gather_start(0)
-            dispatch_own(l + 1, 0, base + 2 * N_Z)
-
-        def combine_second(k, carry):
-            combine_step(l, 1, k, False)
-            return carry
-        lax.fori_loop(0, N_Z, combine_second, 0)
-        if not last:
-            dispatch_rest(l + 1, 0, base + 2 * N_Z + 1)
-        finish(1)
-        if not last:
-            gather_start(1)
+        lax.fori_loop(1, N_Z, rest_ffn, 0)
+    l, m = turns[-1]
+
+    def last_sums(k, carry):
+        combine_step(l, m, k, False)
+        return carry
+    lax.fori_loop(0, N_Z, last_sums, 0)
+    finish(m)
 
     results = [pltpu.make_async_copy(col.at[m, iz], out.at[m], load_sem.at[m, 0]) for m in range(n_micro)]
     for copy in results:
         copy.start()
     for slot in range(SEND_SLOTS):
         for r in range(1, N_PEER):
-            d_copy(0, 0, slot, r).wait_send()
-            r_copy(0, 0, slot, r).wait_send()
+            d_copy(0, iz, slot, r).wait_send()
+            r_copy(0, iz, slot, r).wait_send()
     for k in range(N_Z - 1):
         part_sent(0, row_of(k))
     for l in range(n_layers):
         for a in range(3):
             cross_copy(l, a).wait_send()
+    for t in range(1, N_Z):
+        table_copy(t).wait_send()
     for copy in results:
         copy.wait()
 
@@ -334,16 +359,15 @@
         capacity = capacity_of(tok_mb, top_k, experts)
         block = 2 * exp_dev * capacity
         slots = slot_table(expert_ids, experts, capacity)
-        routes = jnp.concatenate([slots.astype(jnp.float32), gate_vals], axis=-1)
-        routes = lax.all_gather(routes, "ez", axis=2)
-        slots = routes[..., :top_k].astype(jnp.int32) - lax.axis_index("ez") * (N_PEER * block)
-        gates = routes[..., top_k:]
+        pad = ((0, 0), (0, 0), (0, 0), (0, 8 - top_k))
+        routes = jnp.concatenate([jnp.pad(slots.astype(jnp.float32), pad), jnp.pad(gate_vals, pad)], axis=-1)
+        routes = jnp.transpose(routes, (1, 0, 3, 2))
         vmem, any_space = pl.BlockSpec(memory_space=pltpu.VMEM), pl.BlockSpec(memory_space=pl.ANY)
         bf16, f32, dma = jnp.bfloat16, jnp.float32, pltpu.SemaphoreType.DMA
         rows_shape = jax.ShapeDtypeStruct((n_micro, N_Z, N_PEER, block, hidden), bf16)
         outs = pl.pallas_call(
-            functools.partial(moe_kernel, capacity),
-            in_specs=[any_space, vmem, vmem, vmem, any_space, any_space, any_space],
+            functools.partial(moe_kernel, capacity, top_k),
+            in_specs=[any_space, vmem, any_space, any_space, any_space],
             out_specs=[any_space] * 7,
             out_shape=[
                 jax.ShapeDtypeStruct(tokens_in.shape, bf16),
@@ -366,6 +390,7 @@
                 pltpu.VMEM((tok_mb, hidden), f32),
                 pltpu.VMEM((tok_mb, N_PEER * block), bf16),
                 pltpu.VMEM((tok_mb, N_PEER * block), bf16),
+                pltpu.VMEM((N_Z,) + routes.shape, f32),
                 dma((n_micro, N_Z - 1)),
                 dma((n_micro, N_Z)),
                 dma((SEND_SLOTS, N_PEER)),
@@ -376,13 +401,15 @@
                 dma((n_micro, 5)),
                 dma((n_layers, 3)),
                 dma((n_layers, 3)),
+                dma((N_Z - 1,)),
+                dma((N_Z,)),
                 dma((3, 2)),
                 dma(()),
                 dma(()),
             ],
             compiler_params=pltpu.CompilerParams(collective_id=0, has_side_effects=True, vmem_limit_bytes=VMEM_LIMIT),
             name="moe_layers",
-        )(tokens_in, jnp.swapaxes(slots, -1, -2), slots, gates, w_up1, w_up3, w_down)
+        )(tokens_in, routes, w_up1, w_up3, w_down)
         return outs[0]
 
     return jax.shard_map(device_body, mesh=mesh, in_specs=(tok_spec, route_spec, route_spec, weight_spec, weight_spec, weight_spec), out_specs=tok_spec, check_vma=False)

time: 1040 us -> 961 us (0.924)
  Pallas kernels: 999 us -> 951 us
  blocking collectives: 15.5 us -> 0 us
    pallas_call x1, Pallas kernels: 999 us -> 951 us  [device_body(): pl.pallas_call(functools.partial(moe_kernel, capacity, top_k), in_specs=[...]
    all_gather x1 -> x0, blocking collectives: 15.5 us -> none  [device_body(): routes = lax.all_gather(routes, 'ez', axis=2)]
where the time goes in v4:
time: 961 us; the launch traced here: 959 us
  Pallas kernels  951 us (99%)
    pallas_call x1, Pallas kernels, device_body(): pl.pallas_call(functools.partial(moe_kernel, capacity, top_k), in_specs=[...  951 us

profile of v4, /device:TPU:0, one launch (start us, length us, event | category | flops | bytes accessed | tf_op | source)
XLA Modules:
  0.0 958.9 jit_solution(9043192878802776946)
XLA Ops:
  0.0 0.0 copy-start
  0.0 0.8 copy.17
  0.8 0.7 copy.21
  1.6 0.2 convert_reduce_fusion
  1.8 2.4 reduce-window.6
  4.2 0.3 slice_reduce_fusion
  4.6 0.1 fusion
  4.7 0.2 select_reduce_fusion
  5.0 0.0 copy-done
  5.0 0.6 fusion.1.routes_in
  5.6 950.7 %moe_layers.1 = (bf16[2,256,1536]{2,1,0:T(8,128)(2,1)}, bf16[2,4,4,192,1536]{4,3,2,1,0:T(8,128)(2,1)}, bf16[2,4,4,192,1536]{4,3,2,1,0:T(8,128)(2,1)}, f32[2,5,25...) custom-call(bf16[2,256,1536]{2,1,0:T(8,128)(2,1)} %tok_in.1, ...), custom_call_target="tpu_custom_call" | custom-call | tf_op jit(solution)/shard_map/moe_layers/pallas_call | solution.py:368
  956.3 2.7 copy.33
  (4 shorter events, 0.1 us)
Async XLA Ops:
  0.0 5.0 copy-start

commit v5 on v3

--- a/solution.py
+++ b/solution.py
@@ -32,7 +32,7 @@
 def moe_kernel(capacity, top_k, tok_in, routes_in, w_up1, w_up3, w_down,
                out, d_land, r_land, c_land, x_up1, x_up3, x_down,
                col, d_buf, r_buf, part, v_up1, v_up3, v_down, stage, sum_stage, w_hi, w_lo, routes, routes_near,
-               swap_send, ag_send, ag_recv, d_send, d_recv, r_send, r_recv, c_send, c_recv, x_send, x_recv,
+               raw_send, raw_recv, ag_send, ag_recv, d_send, d_recv, r_send, r_recv, c_send, c_recv, x_send, x_recv,
                t_send, t_recv, n_send, n_recv, load_sem, copy_sem, self_sem):
     n_micro, n_layers = routes_in.shape[:2]
     tok_mb = routes_in.shape[3]
@@ -102,39 +102,23 @@
         for z in range(N_Z):
             remote(routes_in, routes_near.at[z], n_send.at[0], n_recv.at[z], partner).wait_recv()
 
-    def swap_copy(m):
-        return remote(col.at[m, 0, iz], col.at[m, 1, iz], swap_send.at[m], ag_recv.at[m, 1, iz], peer(near_axis(iz)))
-
-    def gather_copy(m, t, s, to_inner, sem):
-        return remote(col.at[m, t, s], col.at[m, t, s], ag_send.at[m, t, sem], ag_recv.at[m, t, s], peer(0, inner_z if to_inner else outer_z))
-
-    def gather_wait(m, t, s):
-        remote(col.at[m, t, s], col.at[m, t, s], ag_send.at[m, t, 0], ag_recv.at[m, t, s], partner).wait_recv()
-
-    def gather_start(m, t):
-        @pl.when(is_mid)
-        def _():
-            gather_copy(m, t, iz, False, 1).start()
-        gather_copy(m, t, iz, True, 0).start()
-
-    def pump(m, j):
-        s = near_row(j)
-        for t in range(2):
-            gather_wait(m, t, s)
-
-            @pl.when(is_mid)
-            def _():
-                gather_copy(m, t, s, j == 0, 2 + j).start()
-
-    def gather_sent(m):
-        swap_copy(m).wait_send()
-        for t in range(2):
-            gather_copy(m, t, iz, True, 0).wait_send()
-
-            @pl.when(is_mid)
-            def _():
-                for sem in range(1, 2 + N_Z - 1):
-                    gather_copy(m, t, iz, False, sem).wait_send()
+    def gather_copy(m, t):
+        return remote(col.at[m, 0, iz], col.at[m, 0, iz], ag_send.at[m, t - 1], ag_recv.at[m, iz], peer(0, (iz + t) % N_Z))
+
+    def gather_wait(m, s):
+        remote(col.at[m, 0, s], col.at[m, 0, s], ag_send.at[m, 0], ag_recv.at[m, s], partner).wait_recv()
+
+    def raw_copy(m, s):
+        return remote(col.at[m, 0, s], col.at[m, 1, s], raw_send.at[m, s], raw_recv.at[m, s], peer(near_axis(s)))
+
+    def raw_sent(m):
+        for z in range(N_Z):
+            raw_copy(m, z).wait_send()
+
+    def share(m):
+        for t in (2, 1, 3):
+            gather_copy(m, t).start()
+        raw_copy(m, iz).start()
 
     def d_self(m, t, s, slot):
         return pltpu.make_async_copy(d_buf.at[slot, 0], d_land.at[m, s, t], self_sem)
@@ -170,20 +154,19 @@
         d_self(m, t, s, slot).start()
         d_self(m, t, s, slot).wait()
 
-    def dispatch_near(l, m, count):
-        gather_wait(m, 1, iz)
-        gather_start(m, 1)
-        dispatch(l, m, 1, iz, count)
-
-    def dispatch_row(l, m, j, count):
-        for t in range(2):
-            dispatch(l, m, t, near_row(j), count + t)
-
-    def dispatch_rest(l, m, count):
-        def body(j, carry):
-            dispatch_row(l, m, j, count + 2 * j)
-            return carry
-        lax.fori_loop(0, N_Z - 1, body, 0)
+    def dispatch_held(l, m, s, count):
+        dispatch(l, m, 0, s, count)
+
+    def dispatch_arrived(l, m, j, count):
+        s = near_row(j)
+        gather_wait(m, s)
+        raw_copy(m, s).start()
+        dispatch_held(l, m, s, count + 1 + j)
+
+    def dispatch_near(l, m, j, count):
+        s = jnp.where(j == 0, iz, near_row(j - 1))
+        raw_copy(m, s).wait_recv()
+        dispatch(l, m, 1, s, count + N_Z + j)
 
     def ffn(l, m, k, count):
         s = row_of(k)
@@ -280,16 +263,10 @@
             def _():
                 forward(m, step)
 
-    def intake_step(l, m, k, count):
-        @pl.when(k == 0)
-        def _():
-            dispatch_near(l, m, count)
-        for j in range(N_Z - 1):
-            @pl.when(k == j + 1)
-            def _():
-                pump(m, j)
-
     def finish(m):
+        for t in range(1, N_Z):
+            gather_copy(m, t).wait_send()
+
         @pl.when(is_mid)
         def _():
             chain_arrival(m, 2)
@@ -297,10 +274,6 @@
         chain_arrival(m, 4)
         total = part[iz] + sum_stage[...]
         col[m, 0, iz] = (col[m, 0, iz].astype(jnp.float32) + ROUTE_SCALE * total).astype(jnp.bfloat16)
-
-    def share(m):
-        swap_copy(m).start()
-        gather_start(m, 0)
 
     sources = (w_up1, w_up3, w_down)
     crossed = (x_up1, x_up3, x_down)
@@ -334,62 +307,72 @@
         table_copy(t).start()
     for t in range(N_Z):
         near_table_copy(t).start()
-    for m in range(n_micro):
-        first_load[m].wait()
-        swap_copy(m).start()
-        if m == 0:
-            gather_start(0, 0)
+    first_load[0].wait()
+    share(0)
     for l in range(n_layers):
         for a in range(3):
             cross_copy(l, a).start()
     routes[iz] = routes_in[...]
+    first_load[1].wait()
     tables_wait()
-    dispatch(0, 0, 0, iz, 0)
-    dispatch_near(0, 0, 1)
-    gather_start(1, 0)
-    for j in range(N_Z - 1):
-        pump(0, j)
-        dispatch_row(0, 0, j, 2 + 2 * j)
+    dispatch_held(0, 0, iz, 0)
+    share(1)
+
+    def first_rows(j, carry):
+        dispatch_near(0, 0, j, 0)
+
+        @pl.when(j < N_Z - 1)
+        def _():
+            dispatch_arrived(0, 0, j, 0)
+        return carry
+    lax.fori_loop(0, N_Z, first_rows, 0)
     weights_start(0)
-    for l in range(n_layers):
-        last = l == n_layers - 1
-        d_base, r_base = l * 4 * N_Z, l * 2 * N_Z
-        d_other, d_next = d_base + 2 * N_Z, d_base + 4 * N_Z
-        dispatch(l, 1, 0, iz, d_other)
-        weights_wait(l)
-        gather_sent(0)
-
-        def ffn_first(k, carry):
-            ffn(l, 0, k, r_base + k)
-            intake_step(l, 1, k, d_other + 1)
+    weights_wait(0)
+
+    def first_ffn(k, carry):
+        ffn(0, 0, k, k)
+        return carry
+    lax.fori_loop(0, N_Z, first_ffn, 0)
+    turns = [(l, m) for l in range(n_layers) for m in range(n_micro)]
+    for turn in range(1, len(turns)):
+        (l, m), (l_prev, m_prev) = turns[turn], turns[turn - 1]
+        d_base, r_base = turn * 2 * N_Z, turn * N_Z
+        raw_sent(m_prev)
+        if m == 0:
+            weights_start(l)
+        dispatch_held(l, m, iz, d_base)
+
+        def sums_and_rows(k, carry):
+            combine_step(l_prev, m_prev, k, turn == 1)
+
+            @pl.when(k < N_Z - 1)
+            def _():
+                dispatch_arrived(l, m, k, d_base)
             return carry
-        lax.fori_loop(0, N_Z, ffn_first, 0)
-        dispatch_rest(l, 1, d_other + 2)
-        gather_sent(1)
-
-        def ffn_second(k, carry):
-            ffn(l, 1, k, r_base + N_Z + k)
-            combine_step(l, 0, k, l == 0)
+        lax.fori_loop(0, N_Z, sums_and_rows, 0)
+
+        def near_rows(j, carry):
+            dispatch_near(l, m, j, d_base)
             return carry
-        lax.fori_loop(0, N_Z, ffn_second, 0)
-        if not last:
-            weights_start(l + 1)
-        finish(0)
-        if not last:
-            share(0)
-            dispatch(l + 1, 0, 0, iz, d_next)
-
-        def combine_second(k, carry):
-            combine_step(l, 1, k, False)
-            if not last:
-                intake_step(l + 1, 0, k, d_next + 1)
+        lax.fori_loop(0, N_Z, near_rows, 0)
+        finish(m_prev)
+        if l_prev < n_layers - 1:
+            share(m_prev)
+        if m == 0:
+            weights_wait(l)
+
+        def turn_ffn(k, carry):
+            ffn(l, m, k, r_base + k)
             return carry
-        lax.fori_loop(0, N_Z, combine_second, 0)
-        if not last:
-            dispatch_rest(l + 1, 0, d_next + 2)
-        finish(1)
-        if not last:
-            share(1)
+        lax.fori_loop(0, N_Z, turn_ffn, 0)
+    l, m = turns[-1]
+    raw_sent(m)
+
+    def last_sums(k, carry):
+        combine_step(l, m, k, False)
+        return carry
+    lax.fori_loop(0, N_Z, last_sums, 0)
+    finish(m)
 
     results = [pltpu.make_async_copy(col.at[m, 0, iz], out.at[m], load_sem.at[m, 0]) for m in range(n_micro)]
     for copy in results:
@@ -459,9 +442,10 @@
                 pltpu.VMEM((tok_mb, N_PEER * block), bf16),
                 pltpu.VMEM((N_Z,) + routes.shape, f32),
                 pltpu.VMEM((N_Z,) + routes.shape, f32),
-                dma((n_micro,)),
-                dma((n_micro, 2, N_Z + 1)),
-                dma((n_micro, 2, N_Z)),
+                dma((n_micro, N_Z)),
+                dma((n_micro, N_Z)),
+                dma((n_micro, N_Z - 1)),
+                dma((n_micro, N_Z)),
                 dma((D_SLOTS,)),
                 dma((n_micro, N_Z, 2)),
                 dma((R_SLOTS, N_PEER)),

time: 1090 us -> 916 us (0.84)
  Pallas kernels: 1080 us -> 906 us
    pallas_call x1, Pallas kernels: 1080 us -> 906 us  [device_body(): pl.pallas_call(functools.partial(moe_kernel, capacity, top_k), in_specs=[...]
where the time goes in v5:
time: 916 us; the launch traced here: 914 us
  Pallas kernels  906 us (99%)
    pallas_call x1, Pallas kernels, device_body(): pl.pallas_call(functools.partial(moe_kernel, capacity, top_k), in_specs=[...  906 us

profile of v5, /device:TPU:0, one launch (start us, length us, event | category | flops | bytes accessed | tf_op | source)
XLA Modules:
  0.0 914.1 jit_solution(16431361640939572351)
XLA Ops:
  0.0 0.0 copy-start
  0.0 0.8 copy.17
  0.8 0.7 copy.21
  1.6 0.2 convert_reduce_fusion
  1.8 2.4 reduce-window.6
  4.2 0.3 slice_reduce_fusion
  4.6 0.1 fusion
  4.7 0.2 select_reduce_fusion
  5.0 0.0 copy-done
  5.0 0.6 fusion.1.routes_in
  5.6 905.8 %moe_layers.1 = (bf16[2,256,1536]{2,1,0:T(8,128)(2,1)}, bf16[2,4,4,192,1536]{4,3,2,1,0:T(8,128)(2,1)}, bf16[2,4,4,192,1536]{4,3,2,1,0:T(8,128)(2,1)}, f32[2,5,25...) custom-call(bf16[2,256,1536]{2,1,0:T(8,128)(2,1)} %tok_in.1, ...), custom_call_target="tpu_custom_call" | custom-call | tf_op jit(solution)/shard_map/moe_layers/pallas_call | solution.py:418
  911.4 2.7 copy.33
  (4 shorter events, 0.1 us)
Async XLA Ops:
  0.0 5.0 copy-start

commit v6 on v5

--- a/solution.py
+++ b/solution.py
@@ -11,8 +11,8 @@
 MESH_AXES = ("ez", "ey", "ex")
 N_Z = 4
 N_PEER = 4
-D_SLOTS = 6
-R_SLOTS = 3
+D_SLOTS = 4
+R_SLOTS = 4
 VMEM_LIMIT = 67043328
 COLUMN = 512
 
@@ -157,16 +157,14 @@
     def dispatch_held(l, m, s, count):
         dispatch(l, m, 0, s, count)
 
-    def dispatch_arrived(l, m, j, count):
-        s = near_row(j)
+    def dispatch_arrived(l, m, s, count):
         gather_wait(m, s)
         raw_copy(m, s).start()
-        dispatch_held(l, m, s, count + 1 + j)
-
-    def dispatch_near(l, m, j, count):
-        s = jnp.where(j == 0, iz, near_row(j - 1))
+        dispatch_held(l, m, s, count)
+
+    def dispatch_near(l, m, s, count):
         raw_copy(m, s).wait_recv()
-        dispatch(l, m, 1, s, count + N_Z + j)
+        dispatch(l, m, 1, s, count)
 
     def ffn(l, m, k, count):
         s = row_of(k)
@@ -319,11 +317,11 @@
     share(1)
 
     def first_rows(j, carry):
-        dispatch_near(0, 0, j, 0)
+        dispatch_near(0, 0, jnp.where(j == 0, iz, near_row(j - 1)), 1 + 2 * j)
 
         @pl.when(j < N_Z - 1)
         def _():
-            dispatch_arrived(0, 0, j, 0)
+            dispatch_arrived(0, 0, near_row(j), 2 + 2 * j)
         return carry
     lax.fori_loop(0, N_Z, first_rows, 0)
     weights_start(0)
@@ -340,19 +338,19 @@
         raw_sent(m_prev)
         if m == 0:
             weights_start(l)
-        dispatch_held(l, m, iz, d_base)
 
         def sums_and_rows(k, carry):
             combine_step(l_prev, m_prev, k, turn == 1)
 
             @pl.when(k < N_Z - 1)
             def _():
-                dispatch_arrived(l, m, k, d_base)
+                dispatch_arrived(l, m, row_of(k), d_base + k)
             return carry
         lax.fori_loop(0, N_Z, sums_and_rows, 0)
+        dispatch_held(l, m, iz, d_base + N_Z - 1)
 
         def near_rows(j, carry):
-            dispatch_near(l, m, j, d_base)
+            dispatch_near(l, m, row_of(j), d_base + N_Z + j)
             return carry
         lax.fori_loop(0, N_Z, near_rows, 0)
         finish(m_prev)

time: 916 us -> 908 us (level); the launches traced: 914 us -> 896 us
  Pallas kernels: 906 us -> 888 us
    pallas_call x1, Pallas kernels: 906 us -> 888 us  [device_body(): pl.pallas_call(functools.partial(moe_kernel, capacity, top_k), in_specs=[...]
where the time goes in v6:
time: 908 us; the launch traced here: 896 us
  Pallas kernels  888 us (98%)
    pallas_call x1, Pallas kernels, device_body(): pl.pallas_call(functools.partial(moe_kernel, capacity, top_k), in_specs=[...  888 us

profile of v6, /device:TPU:0, one launch (start us, length us, event | category | flops | bytes accessed | tf_op | source)
XLA Modules:
  0.0 896.3 jit_solution(16612912861459618009)
XLA Ops:
  0.0 0.0 copy-start
  0.0 0.8 copy.17
  0.8 0.7 copy.21
  1.6 0.2 convert_reduce_fusion
  1.8 2.4 reduce-window.6
  4.2 0.3 slice_reduce_fusion
  4.6 0.1 fusion
  4.7 0.2 select_reduce_fusion
  5.0 0.0 copy-done
  5.0 0.6 fusion.1.routes_in
  5.6 888.0 %moe_layers.1 = (bf16[2,256,1536]{2,1,0:T(8,128)(2,1)}, bf16[2,4,4,192,1536]{4,3,2,1,0:T(8,128)(2,1)}, bf16[2,4,4,192,1536]{4,3,2,1,0:T(8,128)(2,1)}, f32[2,5,25...) custom-call(bf16[2,256,1536]{2,1,0:T(8,128)(2,1)} %tok_in.1, ...), custom_call_target="tpu_custom_call" | custom-call | tf_op jit(solution)/shard_map/moe_layers/pallas_call | solution.py:416
  893.6 2.7 copy.33
  (4 shorter events, 0.1 us)
Async XLA Ops:
  0.0 5.0 copy-start

commit v7 on v6

--- a/solution.py
+++ b/solution.py
@@ -151,8 +151,11 @@
             d_buf[slot, dest] = jnp.dot(pick, tokens, preferred_element_type=jnp.float32).astype(jnp.bfloat16)
             if dest:
                 d_copy(m, t, s, slot).start()
+
+        @pl.when(count % (2 * N_Z) != 0)
+        def _():
+            d_self(m, t, s, slot).wait()
         d_self(m, t, s, slot).start()
-        d_self(m, t, s, slot).wait()
 
     def dispatch_held(l, m, s, count):
         dispatch(l, m, 0, s, count)
@@ -191,8 +194,11 @@
             return carry
         lax.fori_loop(0, 2 * exp_dev, one_expert, 0)
         for i in (3, 1, 2, 0):
+            if i == 0:
+                @pl.when(k != 0)
+                def _():
+                    r_copy(m, s, slot, 0).wait()
             r_copy(m, s, slot, i).start()
-        r_copy(m, s, slot, 0).wait()
 
     def chain_copy(m, s, kind, to_inner):
         return remote(part.at[s], c_land.at[m, kind], c_send.at[s], c_recv.at[m, kind], peer(0, inner_z if to_inner else outer_z))
@@ -324,6 +330,7 @@
             dispatch_arrived(0, 0, near_row(j), 2 + 2 * j)
         return carry
     lax.fori_loop(0, N_Z, first_rows, 0)
+    d_self(0, 0, iz, 0).wait()
     weights_start(0)
     weights_wait(0)
 
@@ -331,6 +338,7 @@
         ffn(0, 0, k, k)
         return carry
     lax.fori_loop(0, N_Z, first_ffn, 0)
+    r_copy(0, iz, 0, 0).wait()
     turns = [(l, m) for l in range(n_layers) for m in range(n_micro)]
     for turn in range(1, len(turns)):
         (l, m), (l_prev, m_prev) = turns[turn], turns[turn - 1]
@@ -353,6 +361,7 @@
             dispatch_near(l, m, row_of(j), d_base + N_Z + j)
             return carry
         lax.fori_loop(0, N_Z, near_rows, 0)
+        d_self(m, 0, iz, 0).wait()
         finish(m_prev)
         if l_prev < n_layers - 1:
             share(m_prev)
@@ -363,6 +372,7 @@
             ffn(l, m, k, r_base + k)
             return carry
         lax.fori_loop(0, N_Z, turn_ffn, 0)
+        r_copy(m, iz, 0, 0).wait()
     l, m = turns[-1]
     raw_sent(m)
 

time: 908 us -> 907 us (level)
  no operation moved by 1% of the time
where the time goes in v7:
time: 907 us; the launch traced here: 896 us
  Pallas kernels  888 us (98%)
    pallas_call x1, Pallas kernels, device_body(): pl.pallas_call(functools.partial(moe_kernel, capacity, top_k), in_specs=[...  888 us

profile of v7, /device:TPU:0, one launch (start us, length us, event | category | flops | bytes accessed | tf_op | source)
XLA Modules:
  0.0 896.3 jit_solution(3875011671065687610)
XLA Ops:
  0.0 0.0 copy-start
  0.0 0.8 copy.17
  0.8 0.7 copy.21
  1.6 0.2 convert_reduce_fusion
  1.8 2.4 reduce-window.6
  4.2 0.3 slice_reduce_fusion
  4.6 0.1 fusion
  4.7 0.2 select_reduce_fusion
  5.0 0.0 copy-done
  5.0 0.6 fusion.1.routes_in
  5.6 888.0 %moe_layers.1 = (bf16[2,256,1536]{2,1,0:T(8,128)(2,1)}, bf16[2,4,4,192,1536]{4,3,2,1,0:T(8,128)(2,1)}, bf16[2,4,4,192,1536]{4,3,2,1,0:T(8,128)(2,1)}, f32[2,5,25...) custom-call(bf16[2,256,1536]{2,1,0:T(8,128)(2,1)} %tok_in.1, ...), custom_call_target="tpu_custom_call" | custom-call | tf_op jit(solution)/shard_map/moe_layers/pallas_call | solution.py:426
  893.6 2.7 copy.33
  (4 shorter events, 0.1 us)
Async XLA Ops:
  0.0 5.0 copy-start
